TPU v7x, 16 devices: a whole 2x2x2 slice. The times are simulated.
16 devices in a mesh: dz: 2 (over z), dy: 2 (over y), dx: 4 (over x, core).
Axes of the slice: x: 2, y: 2, z: 2, core: 2. Of those that a mesh axis runs over, the one named last changes fastest.
Arguments:
- x_one: bfloat16 [32768, 1024], P(('dz', 'dy', 'dx'))
- g_one: bfloat16 [32768, 1024], P(('dz', 'dy', 'dx'))
- x_two: bfloat16 [32768, 1024], P(('dz', 'dy', 'dx'))
- g_two: bfloat16 [32768, 1024], P(('dz', 'dy', 'dx'))
- w_one: bfloat16 [1024, 4096], replicated
- w_two: bfloat16 [4096, 1024], replicated
- w_three: bfloat16 [1024, 4096], replicated
- w_four: bfloat16 [4096, 1024], replicated
Outputs:
- output 1: float32 [1024, 4096], replicated
- output 2: float32 [4096, 1024], replicated
- output 3: float32 [1024, 4096], replicated
- output 4: float32 [4096, 1024], replicated
- output 5: bfloat16 [32768, 1024], P(('dz', 'dy', 'dx'))
- output 6: bfloat16 [32768, 1024], P(('dz', 'dy', 'dx'))
All inputs are finite; a program needn't handle non-finite values.
Results may differ from a plain program's by a relative error of at most 0.00337683.
Values are sent between devices in bfloat16 or wider.
A program may use at most 1 GiB of HBM per device.

v0:
```python
import jax
import jax.numpy as jnp
from jax import lax
from jax.sharding import PartitionSpec as P

GELU_C = 0.7978845608028654
GELU_A = 0.044715


def gelu_value(pre_act):
    pre_f = pre_act.astype(jnp.float32)
    return 0.5 * pre_f * (1.0 + jnp.tanh(GELU_C * (pre_f + GELU_A * pre_f * pre_f * pre_f)))


def gelu_slope(pre_act):
    pre_f = pre_act.astype(jnp.float32)
    tanh_val = jnp.tanh(GELU_C * (pre_f + GELU_A * pre_f * pre_f * pre_f))
    return 0.5 * (1.0 + tanh_val) + 0.5 * pre_f * (1.0 - tanh_val * tanh_val) * GELU_C * (1.0 + 3.0 * GELU_A * pre_f * pre_f)


def mat_tn(left_op, right_op):
    return lax.dot_general(left_op, right_op, (((0,), (0,)), ((), ())), preferred_element_type=jnp.float32)


def mat_nt(left_op, right_op):
    return lax.dot_general(left_op, right_op, (((1,), (1,)), ((), ())), preferred_element_type=jnp.float32)


def local_grads(x_rows, g_rows, w_one, w_two, w_three, w_four):
    pre_one = jnp.dot(x_rows, w_one, preferred_element_type=jnp.float32).astype(jnp.bfloat16)
    act_one = gelu_value(pre_one).astype(jnp.bfloat16)
    act_two = (jnp.dot(act_one, w_two, preferred_element_type=jnp.float32) + x_rows.astype(jnp.float32)).astype(jnp.bfloat16)
    pre_three = jnp.dot(act_two, w_three, preferred_element_type=jnp.float32).astype(jnp.bfloat16)
    act_three = gelu_value(pre_three).astype(jnp.bfloat16)
    grad_four = mat_tn(act_three, g_rows)
    dz_three = (mat_nt(g_rows, w_four) * gelu_slope(pre_three)).astype(jnp.bfloat16)
    grad_three = mat_tn(act_two, dz_three)
    dh_two = (mat_nt(dz_three, w_three) + g_rows.astype(jnp.float32)).astype(jnp.bfloat16)
    grad_two = mat_tn(act_one, dh_two)
    dz_one = (mat_nt(dh_two, w_two) * gelu_slope(pre_one)).astype(jnp.bfloat16)
    grad_one = mat_tn(x_rows, dz_one)
    dx_rows = (mat_nt(dz_one, w_one) + dh_two.astype(jnp.float32)).astype(jnp.bfloat16)
    return (grad_one, grad_two, grad_three, grad_four), dx_rows


def solution(mesh):
    dev_count = mesh.shape["dz"] * mesh.shape["dy"] * mesh.shape["dx"]
    row_spec = P(("dz", "dy", "dx"), None)
    rep_spec = P(None, None)

    def mean_over_devices(grad_sum):
        shard_sum = lax.psum_scatter(grad_sum, "dx", scatter_dimension=0, tiled=True)
        shard_sum = lax.psum_scatter(shard_sum, "dy", scatter_dimension=0, tiled=True)
        shard_sum = lax.psum_scatter(shard_sum, "dz", scatter_dimension=0, tiled=True)
        shard_mean = shard_sum / dev_count
        gathered = lax.all_gather(shard_mean, "dz", axis=0, tiled=True)
        gathered = lax.all_gather(gathered, "dy", axis=0, tiled=True)
        return lax.all_gather(gathered, "dx", axis=0, tiled=True)

    def per_device(x_one, g_one, x_two, g_two, w_one, w_two, w_three, w_four):
        grads_first, dx_first = local_grads(x_one, g_one, w_one, w_two, w_three, w_four)
        grads_second, dx_second = local_grads(x_two, g_two, w_one, w_two, w_three, w_four)
        mean_grads = [mean_over_devices(grad_a + grad_b) for grad_a, grad_b in zip(grads_first, grads_second)]
        return mean_grads[0], mean_grads[1], mean_grads[2], mean_grads[3], dx_first, dx_second

    return jax.shard_map(
        per_device,
        mesh=mesh,
        in_specs=(row_spec, row_spec, row_spec, row_spec, rep_spec, rep_spec, rep_spec, rep_spec),
        out_specs=(rep_spec, rep_spec, rep_spec, rep_spec, row_spec, row_spec),
        check_vma=False,
    )
```

profile of v0, /device:TPU:0, one launch (start us, length us, event | category | flops | bytes accessed | tf_op | source)
XLA Modules:
  0.0 1959.5 jit_solution(5423653539364693565)
XLA Ops:
  7.2 24.4 %convolution_convert_fusion.3 = bf16[2048,4096]{1,0:T(8,128)(2,1)} fusion(bf16[2048,1024]{1,0:T(8,128)(2,1)} %param.8, bf16[1024,4096]{1,0:T(8,128)(2,1)} %param.12), kind=kOutput, calls=%fused_computation.78 | convolution fusion | flops 17188257792 | bytes 29360128 | tf_op jit(solution)/shard_map/dot_general | solution.py:30
  31.7 22.6 %convolution_convert_fusion.1 = bf16[2048,4096]{1,0:T(8,128)(2,1)} fusion(bf16[2048,1024]{1,0:T(8,128)(2,1)} %param.10, bf16[1024,4096]{1,0:T(8,128)(2,1)S(1)} %copy-done), kind=kOutput, calls=%fused_computation.76 | convolution fusion | flops 17188257792 | bytes 29360128 | tf_op jit(solution)/shard_map/dot_general | solution.py:30
  54.3 25.8 %add_convert_fusion.5 = bf16[2048,1024]{1,0:T(8,128)(2,1)} fusion(bf16[2048,1024]{1,0:T(8,128)(2,1)S(1)} %copy-done.2, bf16[4096,1024]{1,0:T(8,128)(2,1)S(1)} %bitcast.51, bf16[2048,4096]{1,0:T(8,128)(2,1)} %convolution_convert_fusion.3), kind=kOutput, calls=%fused_computation.87 | convolution fusion | flops 17270046720 | bytes 33554432 | tf_op jit(solution)/shard_map/dot_general | solution.py:32
  80.1 24.5 %add_convert_fusion.3 = bf16[2048,1024]{1,0:T(8,128)(2,1)S(1)} fusion(bf16[2048,1024]{1,0:T(8,128)(2,1)S(1)} %copy-done.6, bf16[4096,1024]{1,0:T(8,128)(2,1)S(1)} %bitcast.51, bf16[2048,4096]{1,0:T(8,128)(2,1)} %convolution_convert_fusion.1), kind=kOutput, calls=%fused_computation.85 | convolution fusion | flops 17270046720 | bytes 33554432 | tf_op jit(solution)/shard_map/dot_general | solution.py:32
  104.6 21.1 %convolution_convert_fusion = bf16[2048,4096]{1,0:T(8,128)(2,1)} fusion(bf16[2048,1024]{1,0:T(8,128)(2,1)S(1)} %add_convert_fusion.3, bf16[1024,4096]{1,0:T(8,128)(2,1)S(1)} %bitcast.47), kind=kOutput, calls=%fused_computation.75 | convolution fusion | flops 17188257792 | bytes 29360128 | tf_op jit(solution)/shard_map/dot_general | solution.py:33
  125.7 20.6 %convolution_convert_fusion.2 = bf16[2048,4096]{1,0:T(8,128)(2,1)} fusion(bf16[2048,1024]{1,0:T(8,128)(2,1)S(1)} %copy-done.8, bf16[1024,4096]{1,0:T(8,128)(2,1)S(1)} %bitcast.47), kind=kOutput, calls=%fused_computation.77 | convolution fusion | flops 17188257792 | bytes 29360128 | tf_op jit(solution)/shard_map/dot_general | solution.py:33
  146.3 28.2 %fusion.44 = f32[4096,1024]{1,0:T(8,128)} fusion(bf16[2048,1024]{1,0:T(8,128)(2,1)S(1)} %copy-done.1, bf16[2048,4096]{1,0:T(8,128)(2,1)} %convolution_convert_fusion.2), kind=kOutput, calls=%fused_computation.73 | convolution fusion | flops 17263755264 | bytes 37748736 | tf_op jit(solution)/shard_map/dot_general | solution.py:22
  174.4 33.2 %fusion.48 = f32[4096,1024]{1,0:T(8,128)} fusion(f32[4096,1024]{1,0:T(8,128)} %fusion.44, bf16[2048,1024]{1,0:T(8,128)(2,1)S(1)} %copy-done.4, bf16[2048,4096]{1,0:T(8,128)(2,1)} %convolution_convert_fusion), kind=kOutput, calls=%fused_computation.80 | convolution fusion | flops 17267949568 | bytes 54525952 | tf_op jit(solution)/shard_map/dot_general | solution.py:22
  207.6 0.0 reduce-scatter.27.cloned.1.call-start
  207.7 43.3 %fusion.24 = bf16[2048,4096]{1,0:T(8,128)(2,1)} fusion(bf16[2048,4096]{1,0:T(8,128)(2,1)} %convolution_convert_fusion.2, bf16[2048,1024]{1,0:T(8,128)(2,1)} %param.9, bf16[4096,1024]{1,0:T(8,128)(2,1)} %param.15), kind=kOutput, calls=%fused_computation.52 | convolution fusion | flops 17347641344 | bytes 46137344 | tf_op jit(solution)/shard_map/dot_general | solution.py:26
  251.1 23.2 %fusion.65 = f32[1024,4096]{1,0:T(8,128)} fusion(bf16[2048,1024]{1,0:T(8,128)(2,1)S(1)} %copy-done.9, bf16[2048,4096]{1,0:T(8,128)(2,1)} %fusion.24), kind=kOutput, calls=%fused_computation.102 | convolution fusion | flops 17179869184 | bytes 37748736 | tf_op jit(solution)/shard_map/dot_general | solution.py:22
  274.3 42.3 %fusion.12 = bf16[2048,4096]{1,0:T(8,128)(2,1)} fusion(bf16[2048,4096]{1,0:T(8,128)(2,1)} %convolution_convert_fusion, bf16[2048,1024]{1,0:T(8,128)(2,1)S(1)} %copy-done.5, bf16[4096,1024]{1,0:T(8,128)(2,1)} %param.15), kind=kOutput, calls=%fused_computation.40 | convolution fusion | flops 17347641344 | bytes 46137344 | tf_op jit(solution)/shard_map/dot_general | solution.py:26
  316.6 28.2 %convolution_add_fusion = f32[1024,4096]{1,0:T(8,128)} fusion(f32[1024,4096]{1,0:T(8,128)} %fusion.65, bf16[2048,1024]{1,0:T(8,128)(2,1)} %copy-done.7, bf16[2048,4096]{1,0:T(8,128)(2,1)} %fusion.12), kind=kOutput, calls=%fused_computation.79 | convolution fusion | flops 17184063488 | bytes 54525952 | tf_op jit(solution)/shard_map/dot_general | solution.py:22
  344.9 0.0 reduce-scatter.17.cloned.1.call-start
  344.9 24.2 %add_convert_fusion.4 = bf16[2048,1024]{1,0:T(8,128)(2,1)} fusion(bf16[2048,1024]{1,0:T(8,128)(2,1)} %param.9, bf16[2048,4096]{1,0:T(8,128)(2,1)} %fusion.24, bf16[1024,4096]{1,0:T(8,128)(2,1)} %param.14), kind=kOutput, calls=%fused_computation.86 | convolution fusion | flops 17186160640 | bytes 33554432 | tf_op jit(solution)/shard_map/dot_general | solution.py:26
  369.2 43.3 %fusion.31 = bf16[2048,4096]{1,0:T(8,128)(2,1)} fusion(bf16[2048,4096]{1,0:T(8,128)(2,1)} %convolution_convert_fusion.3, bf16[2048,1024]{1,0:T(8,128)(2,1)} %add_convert_fusion.4, bf16[4096,1024]{1,0:T(8,128)(2,1)} %param.13), kind=kOutput, calls=%fused_computation.59 | convolution fusion | flops 17347641344 | bytes 46137344 | tf_op jit(solution)/shard_map/dot_general | solution.py:26
  412.5 23.2 %fusion.64 = f32[4096,1024]{1,0:T(8,128)} fusion(bf16[2048,4096]{1,0:T(8,128)(2,1)} %fusion.31, bf16[2048,1024]{1,0:T(8,128)(2,1)S(1)} %copy-done.3), kind=kOutput, calls=%fused_computation.101 | convolution fusion | flops 17179869184 | bytes 37748736 | tf_op jit(solution)/shard_map/dot_general | solution.py:22
  435.7 20.8 %add_convert_fusion.2 = bf16[2048,1024]{1,0:T(8,128)(2,1)S(1)} fusion(bf16[2048,1024]{1,0:T(8,128)(2,1)} %param.11, bf16[2048,4096]{1,0:T(8,128)(2,1)} %fusion.12, bf16[1024,4096]{1,0:T(8,128)(2,1)S(1)} %bitcast.49), kind=kOutput, calls=%fused_computation.84 | convolution fusion | flops 17186160640 | bytes 33554432 | tf_op jit(solution)/shard_map/dot_general | solution.py:26
  456.5 2.0 copy-done.11
  458.5 42.0 %fusion.19 = bf16[2048,4096]{1,0:T(8,128)(2,1)} fusion(bf16[2048,4096]{1,0:T(8,128)(2,1)} %convolution_convert_fusion.1, bf16[2048,1024]{1,0:T(8,128)(2,1)S(1)} %add_convert_fusion.2, bf16[4096,1024]{1,0:T(8,128)(2,1)} %param.13), kind=kOutput, calls=%fused_computation.47 | convolution fusion | flops 17347641344 | bytes 46137344 | tf_op jit(solution)/shard_map/dot_general | solution.py:26
  500.5 28.5 %add_bitcast_fusion = f32[1024,4096]{0,1:T(8,128)} fusion(f32[4096,1024]{1,0:T(8,128)} %fusion.64, bf16[2048,4096]{1,0:T(8,128)(2,1)} %fusion.19, bf16[2048,1024]{1,0:T(8,128)(2,1)} %param.10), kind=kOutput, calls=%fused_computation.72 | convolution fusion | flops 17184063488 | bytes 54525952 | tf_op jit(solution)/shard_map/dot_general | solution.py:22
  529.1 0.0 reduce-scatter.21.cloned.1.call-start
  529.2 29.2 %fusion.61 = f32[4096,1024]{1,0:T(8,128)} fusion(bf16[2048,1024]{1,0:T(8,128)(2,1)} %add_convert_fusion.4, bf16[2048,4096]{1,0:T(8,128)(2,1)} %convolution_convert_fusion.3), kind=kOutput, calls=%fused_computation.100 | convolution fusion | flops 17263755264 | bytes 37748736 | tf_op jit(solution)/shard_map/dot_general | solution.py:22
  558.3 33.5 %convolution_add_fusion.1 = f32[4096,1024]{1,0:T(8,128)} fusion(f32[4096,1024]{1,0:T(8,128)} %fusion.61, bf16[2048,1024]{1,0:T(8,128)(2,1)S(1)} %copy-done.12, bf16[2048,4096]{1,0:T(8,128)(2,1)} %convolution_convert_fusion.1), kind=kOutput, calls=%fused_computation.81 | convolution fusion | flops 17267949568 | bytes 54525952 | tf_op jit(solution)/shard_map/dot_general | solution.py:22
  592.0 0.5 reduce-scatter.33.cloned.1.call-update
  592.5 0.5 reduce-scatter.29.cloned.1.call-update
  593.1 59.5 %reduce-scatter.17.cloned.1.call-done = f32[256,4096]{0,1:T(8,128)} async-done(((f32[1024,4096]{0,1:T(8,128)}), f32[256,4096]{0,1:T(8,128)}) %reduce-scatter.17.cloned.1.call-update) | async-done | bytes 4194320 | tf_op jit(solution)/shard_map/reduce_scatter | solution.py:52
  652.7 123.5 %reduce-scatter.21.cloned.1.call-done = f32[1024,1024]{1,0:T(8,128)} async-done(((f32[4096,1024]{1,0:T(8,128)}), f32[1024,1024]{1,0:T(8,128)}) %reduce-scatter.21.cloned.1.call-update) | async-done | bytes 4194320 | tf_op jit(solution)/shard_map/reduce_scatter | solution.py:52
  776.3 54.5 %reduce-scatter.33.cloned.1.call-done = f32[512,1024]{1,0:T(8,128)} async-done(((f32[1024,1024]{1,0:T(8,128)}), f32[512,1024]{1,0:T(8,128)}) %reduce-scatter.33.cloned.1.call-update) | async-done | bytes 2097168 | tf_op jit(solution)/shard_map/reduce_scatter | solution.py:53
  830.9 54.5 %reduce-scatter.29.cloned.1.call-done = f32[128,4096]{1,0:T(8,128)} async-done(((f32[256,4096]{1,0:T(8,128)}), f32[128,4096]{1,0:T(8,128)}) %reduce-scatter.29.cloned.1.call-update) | async-done | bytes 2097168 | tf_op jit(solution)/shard_map/reduce_scatter | solution.py:53
  885.4 54.6 %reduce-scatter.19.cloned.1.call-done = f32[128,4096]{0,1:T(8,128)} async-done(((f32[256,4096]{0,1:T(8,128)}), f32[128,4096]{0,1:T(8,128)}) %reduce-scatter.19.cloned.1.call-update) | async-done | bytes 2097168 | tf_op jit(solution)/shard_map/reduce_scatter | solution.py:53
  940.1 2.9 copy.24
  943.0 51.8 %reduce-scatter.23.cloned.1.call-done = f32[512,1024]{1,0:T(8,128)} async-done(((f32[1024,1024]{1,0:T(8,128)}), f32[512,1024]{1,0:T(8,128)}) %reduce-scatter.23.cloned.1.call-update) | async-done | bytes 2097168 | tf_op jit(solution)/shard_map/reduce_scatter | solution.py:53
  994.9 32.1 %reduce-scatter.35.cloned.1.call-done = f32[256,1024]{1,0:T(8,128)} async-done(((f32[512,1024]{1,0:T(8,128)}), f32[256,1024]{1,0:T(8,128)}) %reduce-scatter.35.cloned.1.call-update) | async-done | bytes 1048592 | tf_op jit(solution)/shard_map/reduce_scatter | solution.py:54
  1027.0 2.4 broadcast_multiply_fusion
  1029.5 0.0 all-gather.25.cloned.1.call-start
  1029.5 29.5 %reduce-scatter.39.cloned.1.call-done = f32[64,4096]{1,0:T(8,128)} async-done(((f32[128,4096]{1,0:T(8,128)}), f32[64,4096]{1,0:T(8,128)}) %reduce-scatter.39.cloned.1.call-update) | async-done | bytes 1048592 | tf_op jit(solution)/shard_map/reduce_scatter | solution.py:54
  1059.0 2.3 broadcast_multiply_fusion.2
  1061.3 0.0 all-gather.13.cloned.1.call-start
  1061.4 30.5 %reduce-scatter.37.cloned.1.call-done = f32[64,4096]{1,0:T(8,128)} async-done(((f32[128,4096]{1,0:T(8,128)}), f32[64,4096]{1,0:T(8,128)}) %reduce-scatter.37.cloned.1.call-update) | async-done | bytes 1048592 | tf_op jit(solution)/shard_map/reduce_scatter | solution.py:54
  1091.8 2.3 broadcast_multiply_fusion.3
  1094.1 0.0 all-gather.19.cloned.1.call-start
  1094.2 29.7 %reduce-scatter.25.cloned.1.call-done = f32[256,1024]{1,0:T(8,128)} async-done(((f32[512,1024]{1,0:T(8,128)}), f32[256,1024]{1,0:T(8,128)}) %reduce-scatter.25.cloned.1.call-update) | async-done | bytes 1048592 | tf_op jit(solution)/shard_map/reduce_scatter | solution.py:54
  1123.9 2.3 broadcast_multiply_fusion.1
  1126.3 30.2 %all-gather.31.cloned.1.call-done = f32[512,1024]{1,0:T(8,128)} async-done(((f32[256,1024]{1,0:T(8,128)}), f32[512,1024]{1,0:T(8,128)}) %all-gather.31.cloned.1.call-update) | async-done | bytes 2097168 | tf_op jit(solution)/shard_map/all_gather | solution.py:56
  1156.6 33.0 %all-gather.25.cloned.1.call-done = f32[128,4096]{1,0:T(8,128)} async-done(((f32[64,4096]{1,0:T(8,128)}), f32[128,4096]{1,0:T(8,128)}) %all-gather.25.cloned.1.call-update) | async-done | bytes 2097168 | tf_op jit(solution)/shard_map/all_gather | solution.py:56
  1189.6 33.0 %all-gather.13.cloned.1.call-done = f32[128,4096]{1,0:T(8,128)} async-done(((f32[64,4096]{1,0:T(8,128)}), f32[128,4096]{1,0:T(8,128)}) %all-gather.13.cloned.1.call-update) | async-done | bytes 2097168 | tf_op jit(solution)/shard_map/all_gather | solution.py:56
  1222.6 33.0 %all-gather.19.cloned.1.call-done = f32[512,1024]{1,0:T(8,128)} async-done(((f32[256,1024]{1,0:T(8,128)}), f32[512,1024]{1,0:T(8,128)}) %all-gather.19.cloned.1.call-update) | async-done | bytes 2097168 | tf_op jit(solution)/shard_map/all_gather | solution.py:56
  1255.7 56.4 %all-gather.33.cloned.1.call-done = f32[1024,1024]{1,0:T(8,128)} async-done(((f32[512,1024]{1,0:T(8,128)}), f32[1024,1024]{1,0:T(8,128)}) %all-gather.33.cloned.1.call-update) | async-done | bytes 4194320 | tf_op jit(solution)/shard_map/all_gather | solution.py:57
  1312.1 56.4 %all-gather.27.cloned.1.call-done = f32[256,4096]{1,0:T(8,128)} async-done(((f32[128,4096]{1,0:T(8,128)}), f32[256,4096]{1,0:T(8,128)}) %all-gather.27.cloned.1.call-update) | async-done | bytes 4194320 | tf_op jit(solution)/shard_map/all_gather | solution.py:57
  1368.6 56.6 %all-gather.15.cloned.1.call-done = f32[256,4096]{1,0:T(8,128)} async-done(((f32[128,4096]{1,0:T(8,128)}), f32[256,4096]{1,0:T(8,128)}) %all-gather.15.cloned.1.call-update) | async-done | bytes 4194320 | tf_op jit(solution)/shard_map/all_gather | solution.py:57
  1425.3 56.4 %all-gather.21.cloned.1.call-done = f32[1024,1024]{1,0:T(8,128)} async-done(((f32[512,1024]{1,0:T(8,128)}), f32[1024,1024]{1,0:T(8,128)}) %all-gather.21.cloned.1.call-update) | async-done | bytes 4194320 | tf_op jit(solution)/shard_map/all_gather | solution.py:57
  1481.7 24.4 %add_convert_fusion = bf16[2048,1024]{1,0:T(8,128)(2,1)} fusion(bf16[2048,1024]{1,0:T(8,128)(2,1)} %copy-done.11, bf16[2048,4096]{1,0:T(8,128)(2,1)} %fusion.19, bf16[1024,4096]{1,0:T(8,128)(2,1)} %param.12), kind=kOutput, calls=%fused_computation.82 | convolution fusion | flops 17186160640 | bytes 33554432 | tf_op jit(solution)/shard_map/dot_general | solution.py:26
  1506.2 23.8 %add_convert_fusion.1 = bf16[2048,1024]{1,0:T(8,128)(2,1)} fusion(bf16[2048,1024]{1,0:T(8,128)(2,1)S(1)} %copy-done.10, bf16[2048,4096]{1,0:T(8,128)(2,1)} %fusion.31, bf16[1024,4096]{1,0:T(8,128)(2,1)} %param.12), kind=kOutput, calls=%fused_computation.83 | convolution fusion | flops 17186160640 | bytes 33554432 | tf_op jit(solution)/shard_map/dot_general | solution.py:26
  1530.0 58.4 %all-gather.35.cloned.1.call-done = f32[4096,1024]{1,0:T(8,128)} async-done(((f32[1024,1024]{1,0:T(8,128)}), f32[4096,1024]{1,0:T(8,128)}) %all-gather.35.cloned.1.call-update) | async-done | bytes 16777232 | tf_op jit(solution)/shard_map/all_gather | solution.py:58
  1588.4 106.7 %all-gather.29.cloned.1.call-done = f32[1024,4096]{1,0:T(8,128)} async-done(((f32[256,4096]{1,0:T(8,128)}), f32[1024,4096]{1,0:T(8,128)}) %all-gather.29.cloned.1.call-update) | async-done | bytes 16777232 | tf_op jit(solution)/shard_map/all_gather | solution.py:58
  1695.0 106.7 %all-gather.17.cloned.1.call-done = f32[1024,4096]{1,0:T(8,128)} async-done(((f32[256,4096]{1,0:T(8,128)}), f32[1024,4096]{1,0:T(8,128)}) %all-gather.17.cloned.1.call-update) | async-done | bytes 16777232 | tf_op jit(solution)/shard_map/all_gather | solution.py:58
  1801.7 106.5 %all-gather.23.cloned.1.call-done = f32[4096,1024]{1,0:T(8,128)} async-done(((f32[1024,1024]{1,0:T(8,128)}), f32[4096,1024]{1,0:T(8,128)}) %all-gather.23.cloned.1.call-update) | async-done | bytes 16777232 | tf_op jit(solution)/shard_map/all_gather | solution.py:58
  1908.2 13.0 copy.32
  1921.3 13.7 copy.33
  1935.0 8.5 copy.34
  1943.5 1.6 slice-done.2
  1945.1 1.2 slice-done.3
  1946.3 6.2 copy.35
  (98 shorter events, 1.2 us)
Async XLA Ops:
  7.2 584.8 %reduce-scatter.31.cloned.1.call-start = ((), (), s32[]{:S(2)}) async-start(), calls=%async_computation.28 | async-start | bytes 20971520 | tf_op jit(solution)/shard_map/reduce_scatter | solution.py:52
  7.2 24.5 %copy-start = (bf16[1024,4096]{1,0:T(8,128)(2,1)S(1)}, bf16[1024,4096]{1,0:T(8,128)(2,1)}, u32[]{:S(2)}) copy-start(bf16[1024,4096]{1,0:T(8,128)(2,1)} %param.12) | copy-start | bytes 25165828
  7.2 47.1 %slice-start.12 = ((s8[8388608]{0:T(1024)(128)(4,1)}), s8[4194304]{0:T(1024)(128)(4,1)S(1)}, s32[]{:S(2)}) async-start(s8[8388608]{0:T(1024)(128)(4,1)} %bitcast.50), calls=%async_computation.48 | async-start | bytes 8388608
  31.7 22.6 %slice-start.13 = ((s8[8388608]{0:T(1024)(128)(4,1)}), s8[4194304]{0:T(1024)(128)(4,1)S(1)}, s32[]{:S(2)}) async-start(s8[8388608]{0:T(1024)(128)(4,1)} %bitcast.50), calls=%async_computation.49 | async-start | bytes 8388608
  31.7 22.6 %copy-start.2 = (bf16[2048,1024]{1,0:T(8,128)(2,1)S(1)}, bf16[2048,1024]{1,0:T(8,128)(2,1)}, u32[]{:S(2)}) copy-start(bf16[2048,1024]{1,0:T(8,128)(2,1)} %param.8) | copy-start | bytes 12582916
  54.3 25.8 %copy-start.6 = (bf16[2048,1024]{1,0:T(8,128)(2,1)S(1)}, bf16[2048,1024]{1,0:T(8,128)(2,1)}, u32[]{:S(2)}) copy-start(bf16[2048,1024]{1,0:T(8,128)(2,1)} %param.10) | copy-start | bytes 12582916
  54.3 50.3 %slice-start.8 = ((s8[8388608]{0:T(1024)(128)(4,1)}), s8[4194304]{0:T(1024)(128)(4,1)S(1)}, s32[]{:S(2)}) async-start(s8[8388608]{0:T(1024)(128)(4,1)} %bitcast.46), calls=%async_computation.44 | async-start | bytes 8388608
  80.1 24.5 %slice-start.9 = ((s8[8388608]{0:T(1024)(128)(4,1)}), s8[4194304]{0:T(1024)(128)(4,1)S(1)}, s32[]{:S(2)}) async-start(s8[8388608]{0:T(1024)(128)(4,1)} %bitcast.46), calls=%async_computation.45 | async-start | bytes 8388608
  104.6 21.1 %copy-start.7 = (bf16[2048,1024]{1,0:T(8,128)(2,1)}, bf16[2048,1024]{1,0:T(8,128)(2,1)S(1)}, u32[]{:S(2)}) copy-start(bf16[2048,1024]{1,0:T(8,128)(2,1)S(1)} %add_convert_fusion.3) | copy-start | bytes 12582916
  104.6 21.1 %copy-start.8 = (bf16[2048,1024]{1,0:T(8,128)(2,1)S(1)}, bf16[2048,1024]{1,0:T(8,128)(2,1)}, u32[]{:S(2)}) copy-start(bf16[2048,1024]{1,0:T(8,128)(2,1)} %add_convert_fusion.5) | copy-start | bytes 12582916
  125.7 20.6 %copy-start.1 = (bf16[2048,1024]{1,0:T(8,128)(2,1)S(1)}, bf16[2048,1024]{1,0:T(8,128)(2,1)}, u32[]{:S(2)}) copy-start(bf16[2048,1024]{1,0:T(8,128)(2,1)} %param.9) | copy-start | bytes 12582916
  146.3 28.2 %copy-start.4 = (bf16[2048,1024]{1,0:T(8,128)(2,1)S(1)}, bf16[2048,1024]{1,0:T(8,128)(2,1)}, u32[]{:S(2)}) copy-start(bf16[2048,1024]{1,0:T(8,128)(2,1)} %param.11) | copy-start | bytes 12582916
  207.6 384.9 %reduce-scatter.27.cloned.1.call-start = ((), (), s32[]{:S(2)}) async-start(), calls=%async_computation.23 | async-start | bytes 20971520 | tf_op jit(solution)/shard_map/reduce_scatter | solution.py:52
  207.7 43.4 %copy-start.9 = (bf16[2048,1024]{1,0:T(8,128)(2,1)S(1)}, bf16[2048,1024]{1,0:T(8,128)(2,1)}, u32[]{:S(2)}) copy-start(bf16[2048,1024]{1,0:T(8,128)(2,1)} %add_convert_fusion.5) | copy-start | bytes 12582916
  251.0 23.3 %copy-start.5 = (bf16[2048,1024]{1,0:T(8,128)(2,1)S(1)}, bf16[2048,1024]{1,0:T(8,128)(2,1)}, u32[]{:S(2)}) copy-start(bf16[2048,1024]{1,0:T(8,128)(2,1)} %param.11) | copy-start | bytes 12582916
  344.9 307.7 %reduce-scatter.17.cloned.1.call-start = ((), (), s32[]{:S(2)}) async-start(), calls=%async_computation.12 | async-start | bytes 20971520 | tf_op jit(solution)/shard_map/reduce_scatter | solution.py:52
  344.9 90.8 %slice-start.10 = ((s8[8388608]{0:T(1024)(128)(4,1)}), s8[4194304]{0:T(1024)(128)(4,1)S(1)}, s32[]{:S(2)}) async-start(s8[8388608]{0:T(1024)(128)(4,1)} %bitcast.48), calls=%async_computation.46 | async-start | bytes 8388608
  369.2 43.3 %copy-start.3 = (bf16[2048,1024]{1,0:T(8,128)(2,1)S(1)}, bf16[2048,1024]{1,0:T(8,128)(2,1)}, u32[]{:S(2)}) copy-start(bf16[2048,1024]{1,0:T(8,128)(2,1)} %param.8) | copy-start | bytes 12582916
  369.2 66.5 %slice-start.11 = ((s8[8388608]{0:T(1024)(128)(4,1)}), s8[4194304]{0:T(1024)(128)(4,1)S(1)}, s32[]{:S(2)}) async-start(s8[8388608]{0:T(1024)(128)(4,1)} %bitcast.48), calls=%async_computation.47 | async-start | bytes 8388608
  456.5 2.0 copy-start.11
  529.1 247.1 %reduce-scatter.21.cloned.1.call-start = ((), (), s32[]{:S(2)}) async-start(), calls=%async_computation.17 | async-start | bytes 20971520 | tf_op jit(solution)/shard_map/reduce_scatter | solution.py:52
  529.2 29.2 %copy-start.12 = (bf16[2048,1024]{1,0:T(8,128)(2,1)S(1)}, bf16[2048,1024]{1,0:T(8,128)(2,1)}, u32[]{:S(2)}) copy-start(bf16[2048,1024]{1,0:T(8,128)(2,1)} %copy-done.11) | copy-start | bytes 12582916
  591.9 238.9 %reduce-scatter.33.cloned.1.call-start = ((), (), s32[]{:S(2)}) async-start(), calls=%async_computation.29 | async-start | bytes 6291456 | tf_op jit(solution)/shard_map/reduce_scatter | solution.py:53
  592.5 292.9 %reduce-scatter.29.cloned.1.call-start = ((), (), s32[]{:S(2)}) async-start(), calls=%async_computation.24 | async-start | bytes 6291456 | tf_op jit(solution)/shard_map/reduce_scatter | solution.py:53
  593.0 347.0 %reduce-scatter.19.cloned.1.call-start = ((), (), s32[]{:S(2)}) async-start(), calls=%async_computation.13 | async-start | bytes 6291456 | tf_op jit(solution)/shard_map/reduce_scatter | solution.py:53
  652.7 342.2 %reduce-scatter.23.cloned.1.call-start = ((), (), s32[]{:S(2)}) async-start(), calls=%async_computation.18 | async-start | bytes 6291456 | tf_op jit(solution)/shard_map/reduce_scatter | solution.py:53
  776.2 250.8 %reduce-scatter.35.cloned.1.call-start = ((), (), s32[]{:S(2)}) async-start(), calls=%async_computation.30 | async-start | bytes 3145728 | tf_op jit(solution)/shard_map/reduce_scatter | solution.py:54
  830.8 228.2 %reduce-scatter.39.cloned.1.call-start = ((), (), s32[]{:S(2)}) async-start(), calls=%async_computation.35 | async-start | bytes 3145728 | tf_op jit(solution)/shard_map/reduce_scatter | solution.py:54
  885.4 206.5 %reduce-scatter.37.cloned.1.call-start = ((), (), s32[]{:S(2)}) async-start(), calls=%async_computation.34 | async-start | bytes 3145728 | tf_op jit(solution)/shard_map/reduce_scatter | solution.py:54
  943.0 180.9 %reduce-scatter.25.cloned.1.call-start = ((), (), s32[]{:S(2)}) async-start(), calls=%async_computation.19 | async-start | bytes 3145728 | tf_op jit(solution)/shard_map/reduce_scatter | solution.py:54
  994.8 161.7 %all-gather.31.cloned.1.call-start = ((), (), s32[]{:S(2)}) async-start(), calls=%async_computation.31 | async-start | bytes 3145728 | tf_op jit(solution)/shard_map/all_gather | solution.py:56
  1029.5 160.1 %all-gather.25.cloned.1.call-start = ((), (), s32[]{:S(2)}) async-start(), calls=%async_computation.25 | async-start | bytes 3145728 | tf_op jit(solution)/shard_map/all_gather | solution.py:56
  1061.3 161.2 %all-gather.13.cloned.1.call-start = ((), (), s32[]{:S(2)}) async-start(), calls=%async_computation.14 | async-start | bytes 3145728 | tf_op jit(solution)/shard_map/all_gather | solution.py:56
  1094.1 161.4 %all-gather.19.cloned.1.call-start = ((), (), s32[]{:S(2)}) async-start(), calls=%async_computation.20 | async-start | bytes 3145728 | tf_op jit(solution)/shard_map/all_gather | solution.py:56
  1126.2 185.8 %all-gather.33.cloned.1.call-start = ((), (), s32[]{:S(2)}) async-start(), calls=%async_computation.32 | async-start | bytes 6291456 | tf_op jit(solution)/shard_map/all_gather | solution.py:57
  1156.5 212.0 %all-gather.27.cloned.1.call-start = ((), (), s32[]{:S(2)}) async-start(), calls=%async_computation.26 | async-start | bytes 6291456 | tf_op jit(solution)/shard_map/all_gather | solution.py:57
  1189.6 235.7 %all-gather.15.cloned.1.call-start = ((), (), s32[]{:S(2)}) async-start(), calls=%async_computation.15 | async-start | bytes 6291456 | tf_op jit(solution)/shard_map/all_gather | solution.py:57
  1222.6 259.1 %all-gather.21.cloned.1.call-start = ((), (), s32[]{:S(2)}) async-start(), calls=%async_computation.21 | async-start | bytes 6291456 | tf_op jit(solution)/shard_map/all_gather | solution.py:57
  1255.6 332.8 %all-gather.35.cloned.1.call-start = ((), (), s32[]{:S(2)}) async-start(), calls=%async_computation.33 | async-start | bytes 20971520 | tf_op jit(solution)/shard_map/all_gather | solution.py:58
  1312.1 382.9 %all-gather.29.cloned.1.call-start = ((), (), s32[]{:S(2)}) async-start(), calls=%async_computation.27 | async-start | bytes 20971520 | tf_op jit(solution)/shard_map/all_gather | solution.py:58
  1368.6 433.1 %all-gather.17.cloned.1.call-start = ((), (), s32[]{:S(2)}) async-start(), calls=%async_computation.16 | async-start | bytes 20971520 | tf_op jit(solution)/shard_map/all_gather | solution.py:58
  1425.2 483.0 %all-gather.23.cloned.1.call-start = ((), (), s32[]{:S(2)}) async-start(), calls=%async_computation.22 | async-start | bytes 20971520 | tf_op jit(solution)/shard_map/all_gather | solution.py:58
  1481.7 24.4 %copy-start.10 = (bf16[2048,1024]{1,0:T(8,128)(2,1)S(1)}, bf16[2048,1024]{1,0:T(8,128)(2,1)}, u32[]{:S(2)}) copy-start(bf16[2048,1024]{1,0:T(8,128)(2,1)} %add_convert_fusion.4) | copy-start | bytes 12582916
  1908.2 26.7 %slice-start.4 = ((s8[16777216]{0:T(1024)(128)(4,1)}), s8[4194304]{0:T(1024)(128)(4,1)S(1)}, s32[]{:S(2)}) async-start(s8[16777216]{0:T(1024)(128)(4,1)} %bitcast.44), calls=%async_computation.40 | async-start | bytes 8388608
  1908.2 26.7 %slice-start.5 = ((s8[16777216]{0:T(1024)(128)(4,1)}), s8[4194304]{0:T(1024)(128)(4,1)S(1)}, s32[]{:S(2)}) async-start(s8[16777216]{0:T(1024)(128)(4,1)} %bitcast.44), calls=%async_computation.41 | async-start | bytes 8388608
  1921.2 13.7 slice-start.6
  1921.2 13.7 slice-start.7
  1921.3 22.2 %slice-start = ((s8[16777216]{0:T(1024)(128)(4,1)}), s8[4194304]{0:T(1024)(128)(4,1)S(1)}, s32[]{:S(2)}) async-start(s8[16777216]{0:T(1024)(128)(4,1)} %bitcast.42), calls=%async_computation.36 | async-start | bytes 8388608
  1921.3 22.2 %slice-start.1 = ((s8[16777216]{0:T(1024)(128)(4,1)}), s8[4194304]{0:T(1024)(128)(4,1)S(1)}, s32[]{:S(2)}) async-start(s8[16777216]{0:T(1024)(128)(4,1)} %bitcast.42), calls=%async_computation.37 | async-start | bytes 8388608
  1935.0 10.1 slice-start.2
  1935.0 11.3 slice-start.3
Sparse Core Ops, SparseCore 0:
  207.8 123.3 reduce-scatter.30
  345.0 123.3 reduce-scatter.26
  529.2 123.3 reduce-scatter.16
  655.6 120.5 reduce-scatter.20
  778.3 52.4 reduce-scatter.32
  832.9 52.4 reduce-scatter.28
  887.6 52.4 reduce-scatter.18
  942.4 52.4 reduce-scatter.22
  997.0 29.9 reduce-scatter.34
  1029.1 29.9 reduce-scatter.38
  1061.8 29.9 reduce-scatter.36
  1093.9 29.9 reduce-scatter.24
  1125.4 31.0 all-gather.30
  1158.5 31.0 all-gather.24
  1191.5 31.0 all-gather.12
  1224.5 31.0 all-gather.18
  1257.0 55.0 all-gather.32
  1313.5 55.0 all-gather.26
  1370.1 55.0 all-gather.14
  1426.6 55.0 all-gather.20
  1483.3 105.0 all-gather.34
  1589.9 105.0 all-gather.28
  1696.6 105.0 all-gather.16
  1803.1 105.0 all-gather.22
where the time goes:
time: 1970 us; the launch traced here: 1960 us
  waiting for transfers between devices  1250 us (63%)
  matrix products  630 us (32%)
  local copies, waits for them, and re-layouts  49.2 us (2%)
    all_gather x4, waiting for transfers between devices, mean_over_devices(): return lax.all_gather(gathered, 'dx', axis=0, tiled=True)  378 us
    dot_general x8, matrix products, mat_nt(): lax.dot_general(left_op, right_op, (((1,), (1,)), ((), ())), preferred_el...  264 us
    dot_general x8, matrix products, mat_tn(): lax.dot_general(left_op, right_op, (((0,), (0,)), ((), ())), preferred_el...  227 us
    all_gather x4, waiting for transfers between devices, mean_over_devices(): gathered = lax.all_gather(gathered, 'dy', axis=0, tiled=True)  226 us
    reduce_scatter x4, waiting for transfers between devices, mean_over_devices(): lax.psum_scatter(shard_sum, 'dy', scatter_dimension=0, tiled=True)  215 us
    reduce_scatter x4, waiting for transfers between devices, mean_over_devices(): lax.psum_scatter(grad_sum, 'dx', scatter_dimension=0, tiled=True)  183 us
    all_gather x4, waiting for transfers between devices, mean_over_devices(): gathered = lax.all_gather(shard_mean, 'dz', axis=0, tiled=True)  129 us
    reduce_scatter x4, waiting for transfers between devices, mean_over_devices(): lax.psum_scatter(shard_sum, 'dz', scatter_dimension=0, tiled=True)  122 us
  transfers between devices with their start and end apart: 24, of which 22 were waited for; matrix products, arithmetic and copies ran while one was open for 23% of the time, Pallas kernels for 0%

commit v1 on v0

v1 whole, which is shorter than its diff:
```python
import functools

import jax
import jax.numpy as jnp
from jax import lax
from jax.experimental import pallas as pl
from jax.experimental.pallas import tpu as pltpu
from jax.sharding import PartitionSpec as P


GELU_C = 0.7978845608028654
GELU_A = 0.044715
AXES = ("dz", "dy", "dx")
CHUNK = 256
HALF_STEPS = 8
ROW_BLOCK = 512
VMEM_LIMIT = 67_000_000
A_ROWS = ((0, 40), (40, 40), (80, 48))
B_ROWS = ((0, 48), (48, 40), (88, 40))
SIZES = tuple(a[1] + b[1] for a, b in zip(A_ROWS, B_ROWS))
ORDERS = ((2, 1, 0), (1, 0, 2), (0, 2, 1))


def gelu_value(pre_act):
    pre_f = pre_act.astype(jnp.float32)
    return 0.5 * pre_f * (1.0 + jnp.tanh(GELU_C * (pre_f + GELU_A * pre_f * pre_f * pre_f)))


def mat_tn(left_op, right_op):
    return lax.dot_general(left_op, right_op, (((0,), (0,)), ((), ())), preferred_element_type=jnp.float32)


def mat_nt(left_op, right_op):
    return lax.dot_general(left_op, right_op, (((1,), (1,)), ((), ())), preferred_element_type=jnp.float32)


class Reducer:
    def __init__(self, ua, ub, shard, scratch):
        self.ua, self.ub, self.shard = ua, ub, shard
        (self.acc, self.core_in, self.in_one, self.in_two, self.in_three) = (
            scratch[0:3], scratch[3:6], scratch[6:9], scratch[9:12], scratch[12:15])
        self.own_sem, self.send_sem, self.recv_sem = scratch[15:18]
        dz, dy, dx = lax.axis_index("dz"), lax.axis_index("dy"), lax.axis_index("dx")
        self.core = lax.rem(dx, 2)
        self.bits = (dz, dy, lax.div(dx, 2))
        self.partner = {"dx": dx + 1 - 2 * self.core}
        self.peers = ({"dz": 1 - dz}, {"dy": 1 - dy}, {"dx": lax.rem(dx + 2, 4)})

    def blocks(self, core):
        for part in range(3):
            for source, rows, offset in ((self.ua, A_ROWS[part], 0), (self.ub, B_ROWS[part], A_ROWS[part][1])):
                for index in range(8):
                    zyx = (index // 4, (index // 2) % 2, index % 2)
                    position = tuple(zyx[axis] for axis in ORDERS[part])
                    where = (index * 2) + core
                    yield part, source.at[where, pl.ds(rows[0], rows[1]), :], position, pl.ds(offset, rows[1])

    def begin(self):
        barrier = pltpu.get_barrier_semaphore()
        for device in (self.partner, *self.peers):
            pl.semaphore_signal(barrier, inc=1, device_id=device, device_id_type=pl.DeviceIdType.MESH)
        pl.semaphore_wait(barrier, 4)
        for part, source, (a, b, c), rows in self.blocks(1 - self.core):
            pltpu.make_async_remote_copy(
                src_ref=source, dst_ref=self.core_in[part].at[a, b, c, rows, :],
                send_sem=self.send_sem.at[part], recv_sem=self.recv_sem.at[part],
                device_id=self.partner, device_id_type=pl.DeviceIdType.MESH).start()
        for part, source, (a, b, c), rows in self.blocks(self.core):
            pltpu.make_async_copy(source, self.acc[part].at[a, b, c, rows, :], self.own_sem.at[part]).start()

    def phase_copy(self, phase, part):
        order = ORDERS[part]
        a, b, c = (self.bits[axis] for axis in order)
        acc = self.acc[part]
        if phase == 1:
            source, target = acc.at[1 - a], self.in_one[part]
        elif phase == 2:
            source, target = acc.at[a, 1 - b], self.in_two[part]
        else:
            source, target = acc.at[a, b, 1 - c], self.in_three[part]
        slot = phase * 3 + part
        return pltpu.make_async_remote_copy(
            src_ref=source, dst_ref=target, send_sem=self.send_sem.at[slot], recv_sem=self.recv_sem.at[slot],
            device_id=self.peers[order[phase - 1]], device_id_type=pl.DeviceIdType.MESH)

    def first(self):
        for part in range(3):
            whole = pltpu.make_async_remote_copy(
                src_ref=self.acc[part], dst_ref=self.core_in[part], send_sem=self.send_sem.at[part],
                recv_sem=self.recv_sem.at[part], device_id=self.partner, device_id_type=pl.DeviceIdType.MESH)
            whole.wait_recv()
            whole.wait_send()
            pltpu.make_async_copy(self.acc[part], self.acc[part], self.own_sem.at[part]).wait()
        for part in range(3):
            @pl.loop(0, 4)
            def _(index, part=part):
                a, b = lax.div(index, 2), lax.rem(index, 2)
                self.acc[part][a, b] = self.acc[part][a, b] + self.core_in[part][a, b]

            self.phase_copy(1, part).start()

    def second(self):
        for part in range(3):
            self.phase_copy(1, part).wait()
            a = self.bits[ORDERS[part][0]]
            for b in range(2):
                self.acc[part][a, b] = self.acc[part][a, b] + self.in_one[part][b]
            self.phase_copy(2, part).start()

    def third(self):
        for part in range(3):
            self.phase_copy(2, part).wait()
            a, b = (self.bits[axis] for axis in ORDERS[part][:2])
            self.acc[part][a, b] = self.acc[part][a, b] + self.in_two[part][...]
            self.phase_copy(3, part).start()

    def finish(self):
        for part in range(3):
            self.phase_copy(3, part).wait()
            a, b, c = (self.bits[axis] for axis in ORDERS[part])
            total = (self.acc[part][a, b, c] + self.in_three[part][...]) * (1.0 / 16.0)
            (a0, an), (b0, bn) = A_ROWS[part], B_ROWS[part]
            self.shard[0, 0, a0:a0 + an, :] = total[:an]
            self.shard[0, 1, b0:b0 + bn, :] = total[an:]


def reducer_scratch():
    f32 = jnp.float32
    return [
        *[pltpu.VMEM((2, 2, 2, size, 1024), f32) for size in SIZES],
        *[pltpu.VMEM((2, 2, 2, size, 1024), f32) for size in SIZES],
        *[pltpu.VMEM((2, 2, size, 1024), f32) for size in SIZES],
        *[pltpu.VMEM((2, size, 1024), f32) for size in SIZES],
        *[pltpu.VMEM((size, 1024), f32) for size in SIZES],
        pltpu.SemaphoreType.DMA((3,)),
        pltpu.SemaphoreType.DMA((12,)),
        pltpu.SemaphoreType.DMA((12,)),
    ]


def reduce_kernel(ua, ub, shard, *scratch):
    work = Reducer(ua, ub, shard, scratch)
    work.begin()
    work.first()
    work.second()
    work.third()
    work.finish()


SHARD = jax.ShapeDtypeStruct((1, 2, 128, 1024), jnp.float32)


def reduce_unit(unit, collective_id):
    return pl.pallas_call(
        reduce_kernel,
        out_shape=SHARD,
        in_specs=[pl.BlockSpec(memory_space=pl.ANY)] * 2,
        out_specs=pl.BlockSpec(memory_space=pltpu.VMEM),
        scratch_shapes=reducer_scratch(),
        compiler_params=pltpu.CompilerParams(
            collective_id=collective_id, has_side_effects=True, vmem_limit_bytes=VMEM_LIMIT),
        cost_estimate=pl.CostEstimate(flops=60_000_000_000, bytes_accessed=32 << 20, transcendentals=0),
    )(*unit)


def stage_kernel(rides, schedule, *refs):
    (p_one, p_two, g_one, g_two, at_one, at_two, w_ref), refs = refs[:7], refs[7:]
    if rides:
        (ua_in, ub_in), refs = refs[:2], refs[2:]
    refs = refs[2:] if schedule == "second" else refs
    (dz_one, dz_two, ua, ub), refs = refs[:4], refs[4:]
    if rides:
        shard, refs = refs[0], refs[1:]
    act, refs = refs[0], refs[1:]
    step = pl.program_id(0)
    work = Reducer(ua_in, ub_in, shard, refs) if rides else None

    def ticks(mb):
        if rides:
            for at, action in ((0, work.begin), (3, work.first), (10, work.second), (14, work.third)):
                if at % 2 == mb:
                    pl.when(step == at // 2)(action)

    for mb, (p_ref, g_ref, at_ref, dz_ref) in enumerate(((p_one, g_one, at_one, dz_one), (p_two, g_two, at_two, dz_two))):
        ticks(mb)
        for row in range(0, p_ref.shape[0], ROW_BLOCK):
            rows = pl.ds(row, ROW_BLOCK)
            upstream = mat_nt(g_ref[rows, :], w_ref[...])
            pre = p_ref[rows, :].astype(jnp.float32)
            square = pre * pre
            half = 0.5 + 0.5 * jnp.tanh(pre * (GELU_C + (GELU_C * GELU_A) * square))
            act[rows, :] = (pre * half).astype(jnp.bfloat16)
            slope = half + pre * (half * (1.0 - half)) * (2.0 * GELU_C + (6.0 * GELU_C * GELU_A) * square)
            dz_ref[rows, :] = (upstream * slope).astype(jnp.bfloat16)
        from_act = mat_tn(act[...], g_ref[...]).reshape(ua.shape)
        from_dz = jnp.dot(at_ref[...], dz_ref[...], preferred_element_type=jnp.float32).reshape(ub.shape)
        if mb == 0:
            ua[...] = from_act
            ub[...] = from_dz
        else:
            ua[...] += from_act
            ub[...] += from_dz
    if rides:
        pl.when(step == HALF_STEPS - 1)(work.finish)


def stage(pres, grads, acts_t, weight, second_from=None, ride=None, collective_id=None):
    rows, wide = pres[0].shape
    base = 0 if second_from is None else HALF_STEPS
    resident = pl.Buffered(1)
    column = pl.BlockSpec((rows, CHUNK), lambda c: (0, base + c))
    in_specs = [
        column, column,
        *[pl.BlockSpec((rows, 1024), lambda c: (0, 0), pipeline_mode=resident)] * 2,
        *[pl.BlockSpec((1024, rows), lambda c: (0, 0), pipeline_mode=resident)] * 2,
        pl.BlockSpec((CHUNK, 1024), lambda c: (base + c, 0)),
    ]
    operands = [*pres, *grads, *acts_t, weight]
    any_spec = pl.BlockSpec(memory_space=pl.ANY)
    out_shape = [
        jax.ShapeDtypeStruct((rows, wide), jnp.bfloat16),
        jax.ShapeDtypeStruct((rows, wide), jnp.bfloat16),
        jax.ShapeDtypeStruct((16, 128, 1024), jnp.float32),
        jax.ShapeDtypeStruct((16, 2, 64, 1024), jnp.float32),
    ]
    out_specs = [
        column, column,
        pl.BlockSpec((2, 128, 1024), lambda c: (c, 0, 0)),
        pl.BlockSpec((16, 1, 64, CHUNK), lambda c: (0, c // 4, 0, c % 4)),
    ]
    scratch = [pltpu.VMEM((rows, CHUNK), jnp.bfloat16)]
    params = dict(vmem_limit_bytes=VMEM_LIMIT, dimension_semantics=("arbitrary",))
    if ride is not None:
        operands += list(ride)
        in_specs += [any_spec, any_spec]
        out_shape.append(SHARD)
        out_specs.append(pl.BlockSpec(memory_space=pltpu.VMEM))
        scratch += reducer_scratch()
        params.update(collective_id=collective_id, has_side_effects=True)
    aliases = {}
    if second_from is not None:
        aliases = {len(operands): 0, len(operands) + 1: 1}
        operands += list(second_from)
        in_specs += [any_spec, any_spec]
    flops = 2 * 3 * 2 * rows * 1024 * CHUNK * HALF_STEPS
    out = pl.pallas_call(
        functools.partial(stage_kernel, ride is not None, "second" if second_from is not None else "first"),
        grid=(HALF_STEPS,),
        out_shape=out_shape,
        in_specs=in_specs,
        out_specs=out_specs,
        scratch_shapes=scratch,
        input_output_aliases=aliases,
        compiler_params=pltpu.CompilerParams(**params),
        cost_estimate=pl.CostEstimate(flops=flops, bytes_accessed=80 << 20, transcendentals=0),
    )(*operands)
    unit = (out[2], out[3].reshape(16, 128, 1024))
    return (out[0], out[1]), unit, (out[4] if ride is not None else None)


def assemble_kernel(*refs):
    source, (row_type, col_type) = refs[0], refs[-2:]
    row_type[...] = source[:, 0].reshape(row_type.shape)
    for shard in range(2):
        for side in range(2):
            col_type[shard * 64:(shard + 1) * 64, side * 1024:(side + 1) * 1024] = source[shard, 1, side * 64:(side + 1) * 64, :]


def assemble(gathered, before=None):
    half = 0 if before is None else 1
    operands, in_specs, aliases = [gathered], [pl.BlockSpec((2, 2, 128, 1024), lambda c: (c, 0, 0, 0))], {}
    if before is not None:
        operands += list(before)
        in_specs += [pl.BlockSpec(memory_space=pl.ANY)] * 2
        aliases = {1: 0, 2: 1}
    return pl.pallas_call(
        assemble_kernel,
        grid=(8,),
        out_shape=[jax.ShapeDtypeStruct((4096, 1024), jnp.float32), jax.ShapeDtypeStruct((1024, 4096), jnp.float32)],
        in_specs=in_specs,
        out_specs=[pl.BlockSpec((256, 1024), lambda c: (8 * half + c, 0)), pl.BlockSpec((128, 2048), lambda c: (c, half))],
        input_output_aliases=aliases,
        cost_estimate=pl.CostEstimate(flops=10_000_000, bytes_accessed=32 << 20, transcendentals=0),
    )(*operands)


def solution(mesh):
    row_spec = P(AXES, None)
    rep_spec = P(None, None)

    def forward(x_rows, w_one, w_two, w_three):
        pre_one = jnp.dot(x_rows, w_one, preferred_element_type=jnp.float32).astype(jnp.bfloat16)
        act_one = gelu_value(pre_one).astype(jnp.bfloat16)
        act_two = (jnp.dot(act_one, w_two, preferred_element_type=jnp.float32) + x_rows.astype(jnp.float32)).astype(jnp.bfloat16)
        pre_three = jnp.dot(act_two, w_three, preferred_element_type=jnp.float32).astype(jnp.bfloat16)
        return pre_one, act_two, pre_three

    def through(dz_rows, weight, grad_rows):
        return (mat_nt(dz_rows, weight) + grad_rows.astype(jnp.float32)).astype(jnp.bfloat16)

    def gather(shard):
        return lax.all_gather(shard, AXES, axis=0, tiled=True)

    def whole_step(x_one, g_one, x_two, g_two, w_one, w_two, w_three, w_four):
        pre_a, mid_a, top_a = forward(x_one, w_one, w_two, w_three)
        pre_b, mid_b, top_b = forward(x_two, w_one, w_two, w_three)
        grads = (g_one, g_two)
        mids_t = (mid_a.T, mid_b.T)
        tops = (top_a, top_b)
        dz_three, unit_one, _ = stage(tops, grads, mids_t, w_four)
        dz_three, unit_two, shard_one = stage(tops, grads, mids_t, w_four, dz_three, unit_one, 0)
        whole_one = gather(shard_one)
        dmid = (through(dz_three[0], w_three, g_one), through(dz_three[1], w_three, g_two))
        pres = (pre_a, pre_b)
        xs_t = (x_one.T, x_two.T)
        dz_one, unit_three, shard_two = stage(pres, dmid, xs_t, w_two, None, unit_two, 1)
        whole_two = gather(shard_two)
        dz_one, unit_four, shard_three = stage(pres, dmid, xs_t, w_two, dz_one, unit_three, 2)
        whole_three = gather(shard_three)
        shard_four = reduce_unit(unit_four, 3)
        shard_four, dz_a, dz_b = lax.optimization_barrier((shard_four, dz_one[0], dz_one[1]))
        whole_four = gather(shard_four)
        dx_one, dx_two = through(dz_a, w_one, dmid[0]), through(dz_b, w_one, dmid[1])
        dw_four, dw_three = assemble(whole_two, assemble(whole_one))
        dw_two, dw_one = assemble(whole_four, assemble(whole_three))
        return dw_one, dw_two, dw_three, dw_four, dx_one, dx_two

    return jax.shard_map(
        whole_step,
        mesh=mesh,
        in_specs=(row_spec, row_spec, row_spec, row_spec, rep_spec, rep_spec, rep_spec, rep_spec),
        out_specs=(rep_spec, rep_spec, rep_spec, rep_spec, row_spec, row_spec),
        check_vma=False,
    )
```

time: 1970 us -> 853 us (0.43)
  waiting for transfers between devices: 1250 us -> 69.4 us
  Pallas kernels: 0 us -> 503 us
  matrix products: 630 us -> 246 us
  local copies, waits for them, and re-layouts: 49.2 us -> 13 us
    all_gather x12 -> x4, waiting for transfers between devices: 733 us -> 68.7 us  [gather(): return lax.all_gather(shard, AXES, axis=0, tiled=True)]
    reduce_scatter x12 -> x0, waiting for transfers between devices: 520 us -> none  [the longest x4 215 us: mean_over_devices(): lax.psum_scatter(shard_sum, 'dy', scatter_dimension=0, tiled=True)]
    pallas_call x0 -> x9, Pallas kernels: none -> 503 us  [the longest x4 331 us: stage(): pl.pallas_call(functools.partial(stage_kernel, ride is not None, 'second'...]
    dot_general x14 -> x6, matrix products: 366 us -> 154 us  [the longest x2 58.9 us: forward(): jnp.dot(act_one, w_two, preferred_element_type=jnp.float32)]
    dot_general x8 -> x4, matrix products: 264 us -> 92.6 us  [mat_nt(): lax.dot_general(left_op, right_op, (((1,), (1,)), ((), ())), preferred_el...]
    unnamed x59 -> x16, local copies, waits for them, and re-layouts: 49.2 us -> 13 us
  transfers between devices with their start and end apart: 24 -> 4, of which waited for: 22 -> 2; matrix products, arithmetic and copies ran while one was open for 23% -> 11% of each run, Pallas kernels for 0% -> 39%
where the time goes in v1:
time: 853 us; the launch traced here: 846 us
  Pallas kernels  503 us (59%)
  matrix products  246 us (29%)
  waiting for transfers between devices  69.4 us (8%)
  between operations  14.3 us (2%)
  local copies, waits for them, and re-layouts  13 us (2%)
    pallas_call x4, Pallas kernels, stage(): pl.pallas_call(functools.partial(stage_kernel, ride is not None, 'second'...  331 us
    pallas_call x1, Pallas kernels, reduce_unit(): pl.pallas_call(reduce_kernel, out_shape=SHARD, in_specs=[pl.BlockSpec(mem...  117 us
    dot_general x4, matrix products, mat_nt(): lax.dot_general(left_op, right_op, (((1,), (1,)), ((), ())), preferred_el...  92.6 us
    all_gather x4, waiting for transfers between devices, gather(): return lax.all_gather(shard, AXES, axis=0, tiled=True)  68.7 us
    dot_general x2, matrix products, forward(): jnp.dot(act_one, w_two, preferred_element_type=jnp.float32)  58.9 us
    pallas_call x4, Pallas kernels, assemble(): pl.pallas_call(assemble_kernel, grid=(8,), out_shape=[jax.ShapeDtypeStruc...  55.5 us
    dot_general x2, matrix products, forward(): jnp.dot(act_two, w_three, preferred_element_type=jnp.float32)  49.7 us
    dot_general x2, matrix products, forward(): jnp.dot(x_rows, w_one, preferred_element_type=jnp.float32)  45 us
  transfers between devices with their start and end apart: 4, of which 2 were waited for; matrix products, arithmetic and copies ran while one was open for 11% of the time, Pallas kernels for 39%

profile of v1, /device:TPU:0, one launch (start us, length us, event | category | flops | bytes accessed | tf_op | source)
XLA Modules:
  0.0 845.9 jit_solution(14620723696402770767)
XLA Ops:
  7.2 0.0 all-gather.11.cloned.1.call-start
  7.2 6.5 copy.30
  13.7 0.0 copy-start
  13.7 0.0 copy-start.3
  13.7 24.4 %convolution_convert_fusion.2.refs_1_ = bf16[2048,4096]{1,0:T(8,128)(2,1)} fusion(bf16[2048,1024]{1,0:T(8,128)(2,1)} %param.10, bf16[1024,4096]{1,0:T(8,128)(2,1)} %param.12), kind=kOutput, calls=%fused_computation.24 | convolution fusion | flops 17188257792 | bytes 29360128 | tf_op jit(solution)/shard_map/dot_general | solution.py:292
  38.2 0.0 copy-done
  38.2 0.0 copy-done.3
  38.2 20.6 %convolution_convert_fusion.3.refs_0_ = bf16[2048,4096]{1,0:T(8,128)(2,1)} fusion(bf16[2048,1024]{1,0:T(8,128)(2,1)S(1)} %copy-done, bf16[1024,4096]{1,0:T(8,128)(2,1)S(1)} %copy-done.3), kind=kOutput, calls=%fused_computation.25 | convolution fusion | flops 17188257792 | bytes 29360128 | tf_op jit(solution)/shard_map/dot_general | solution.py:292
  58.7 6.4 copy.28
  65.1 25.0 %add_convert_fusion.4 = bf16[2048,1024]{0,1:T(8,128)(2,1)} fusion(bf16[2048,1024]{0,1:T(8,128)(2,1)} %copy.30, bf16[4096,1024]{1,0:T(8,128)(2,1)} %refs_6_.7, bf16[2048,4096]{1,0:T(8,128)(2,1)} %convolution_convert_fusion.2.refs_1_), kind=kOutput, calls=%fused_computation.30 | convolution fusion | flops 17270046720 | bytes 33554432 | tf_op jit(solution)/shard_map/dot_general | solution.py:294
  90.2 0.0 copy-start.1
  90.2 24.9 %convolution_convert_fusion.refs_1_ = bf16[2048,4096]{1,0:T(8,128)(2,1)} fusion(bf16[2048,1024]{0,1:T(8,128)(2,1)} %add_convert_fusion.4, bf16[1024,4096]{1,0:T(8,128)(2,1)} %param.14), kind=kOutput, calls=%fused_computation.22 | convolution fusion | flops 17188257792 | bytes 29360128 | tf_op jit(solution)/shard_map/dot_general | solution.py:295
  115.1 0.0 copy-done.1
  115.1 33.9 %add_convert_fusion.5 = bf16[2048,1024]{0,1:T(8,128)(2,1)} fusion(bf16[2048,1024]{0,1:T(8,128)(2,1)S(1)} %copy-done.1, bf16[4096,1024]{1,0:T(8,128)(2,1)} %refs_6_.7, bf16[2048,4096]{1,0:T(8,128)(2,1)} %convolution_convert_fusion.3.refs_0_), kind=kOutput, calls=%fused_computation.31 | convolution fusion | flops 17270046720 | bytes 33554432 | tf_op jit(solution)/shard_map/dot_general | solution.py:294
  148.9 24.8 %convolution_convert_fusion.1.refs_0_ = bf16[2048,4096]{1,0:T(8,128)(2,1)} fusion(bf16[2048,1024]{0,1:T(8,128)(2,1)} %add_convert_fusion.5, bf16[1024,4096]{1,0:T(8,128)(2,1)} %param.14), kind=kOutput, calls=%fused_computation.23 | convolution fusion | flops 17188257792 | bytes 29360128 | tf_op jit(solution)/shard_map/dot_general | solution.py:295
  173.7 71.0 %shard_map.127 = (bf16[2048,4096]{1,0:T(8,128)(2,1)}, bf16[2048,4096]{1,0:T(8,128)(2,1)}, f32[16,128,1024]{2,1,0:T(8,128)}, f32[16,2,64,1024]{3,2,1,0:T(8,128)}) custom-call(bf16[2048,4096]{1,0:T(8,128)(2,1)} %convolution_convert_fusion.1.refs_0_, bf16[2048,4096]{1,0:T(8,128)(2,1)} %convolution_convert_fusion.refs_1_, bf16[2048,1024]{1,0:T(8,128)(2,1)} %refs_2_.3, ...), custom_call_target="tpu_custom_call" | custom-call | flops 51539607552 | bytes 83886080 | tf_op jit(solution)/shard_map/pallas_call | solution.py:246
  244.7 87.8 %shard_map.128 = (bf16[2048,4096]{1,0:T(8,128)(2,1)}, bf16[2048,4096]{1,0:T(8,128)(2,1)}, f32[16,128,1024]{2,1,0:T(8,128)}, f32[16,2,64,1024]{3,2,1,0:T(8,128)}, f32[1,2,128,1024]{3,2,1,0:T(8,128)}) custom-call(bf16[2048,4096]{1,0:T(8,128)(2,1)} %convolution_convert_fusion.1.refs_0_, ...), custom_call_target="tpu_custom_call", output_to_operand_aliasing={{0}: (9, {}), {1}: (10, {})} | custom-call | flops 51539607552 | bytes 83886080 | tf_op jit(solution)/shard_map/pallas_call | solution.py:246
  332.5 0.0 all-gather.11.cloned.1.call-update
  332.5 0.0 all-gather.7.cloned.1.call-start
  332.5 0.0 copy-start.2
  332.6 0.0 copy-start.5
  332.6 25.5 %add_convert_fusion.2.refs_3_ = bf16[2048,1024]{1,0:T(8,128)(2,1)} fusion(bf16[2048,1024]{1,0:T(8,128)(2,1)} %refs_3_.3, bf16[2048,4096]{1,0:T(8,128)(2,1)} %get-tuple-element.41, bf16[1024,4096]{1,0:T(8,128)(2,1)} %param.14), kind=kOutput, calls=%fused_computation.28 | convolution fusion | flops 17186160640 | bytes 33554432 | tf_op jit(solution)/shard_map/dot_general | solution.py:34
  358.0 0.0 copy-done.2
  358.0 0.0 copy-done.5
  358.1 21.5 %add_convert_fusion.3.refs_2_ = bf16[2048,1024]{1,0:T(8,128)(2,1)} fusion(bf16[2048,1024]{1,0:T(8,128)(2,1)S(1)} %copy-done.5, bf16[2048,4096]{1,0:T(8,128)(2,1)} %get-tuple-element.40, bf16[1024,4096]{1,0:T(8,128)(2,1)S(1)} %copy-done.2), kind=kOutput, calls=%fused_computation.29 | convolution fusion | flops 17186160640 | bytes 33554432 | tf_op jit(solution)/shard_map/dot_general | solution.py:34
  379.5 87.4 %shard_map.129 = (bf16[2048,4096]{1,0:T(8,128)(2,1)}, bf16[2048,4096]{1,0:T(8,128)(2,1)}, f32[16,128,1024]{2,1,0:T(8,128)}, f32[16,2,64,1024]{3,2,1,0:T(8,128)}, f32[1,2,128,1024]{3,2,1,0:T(8,128)}) custom-call(bf16[2048,4096]{1,0:T(8,128)(2,1)} %convolution_convert_fusion.3.refs_0_, bf16[2048,4096]{1,0:T(8,128)(2,1)} %convolution_convert_fusion.2.refs_1_, ...), custom_call_target="tpu_custom_call" | custom-call | flops 51539607552 | bytes 83886080 | tf_op jit(solution)/shard_map/pallas_call | solution.py:246
  466.9 84.6 %shard_map.130 = (bf16[2048,4096]{1,0:T(8,128)(2,1)}, bf16[2048,4096]{1,0:T(8,128)(2,1)}, f32[16,128,1024]{2,1,0:T(8,128)}, f32[16,2,64,1024]{3,2,1,0:T(8,128)}, f32[1,2,128,1024]{3,2,1,0:T(8,128)}) custom-call(bf16[2048,4096]{1,0:T(8,128)(2,1)} %convolution_convert_fusion.3.refs_0_, ...), custom_call_target="tpu_custom_call", output_to_operand_aliasing={{0}: (9, {}), {1}: (10, {})} | custom-call | flops 51539607552 | bytes 83886080 | tf_op jit(solution)/shard_map/pallas_call | solution.py:246
  551.6 0.0 all-gather.7.cloned.1.call-update
  551.6 0.0 all-gather.9.cloned.1.call-start
  551.7 0.7 all-gather.9.cloned.1.call-update
  552.3 0.0 all-gather.5.cloned.1.call-start
  552.4 116.5 %shard_map.131 = f32[1,2,128,1024]{3,2,1,0:T(8,128)} custom-call(f32[16,128,1024]{2,1,0:T(8,128)} %get-tuple-element.48.ua, f32[16,128,1024]{2,1,0:T(8,128)} %bitcast.30), custom_call_target="tpu_custom_call" | custom-call | flops 60000002048 | bytes 33554432 | tf_op jit(solution)/shard_map/pallas_call | solution.py:154
  668.9 0.0 all-gather.5.cloned.1.call-update
  668.9 0.0 copy-start.4
  668.9 0.0 copy-start.6
  668.9 24.2 %add_convert_fusion = bf16[2048,1024]{1,0:T(8,128)(2,1)} fusion(bf16[2048,1024]{1,0:T(8,128)(2,1)} %add_convert_fusion.2.refs_3_, bf16[2048,4096]{1,0:T(8,128)(2,1)} %get-tuple-element.65, bf16[1024,4096]{1,0:T(8,128)(2,1)} %param.12), kind=kOutput, calls=%fused_computation.26 | convolution fusion | flops 17186160640 | bytes 33554432 | tf_op jit(solution)/shard_map/dot_general | solution.py:34
  693.2 0.0 copy-done.4
  693.2 0.0 copy-done.6
  693.2 21.5 %add_convert_fusion.1 = bf16[2048,1024]{1,0:T(8,128)(2,1)} fusion(bf16[2048,1024]{1,0:T(8,128)(2,1)S(1)} %copy-done.6, bf16[2048,4096]{1,0:T(8,128)(2,1)} %get-tuple-element.64, bf16[1024,4096]{1,0:T(8,128)(2,1)S(1)} %copy-done.4), kind=kOutput, calls=%fused_computation.27 | convolution fusion | flops 17186160640 | bytes 33554432 | tf_op jit(solution)/shard_map/dot_general | solution.py:34
  714.6 0.0 all-gather.11.cloned.1.call-done.refs_0_
  714.6 13.9 %shard_map.134 = (f32[4096,1024]{1,0:T(8,128)}, f32[1024,4096]{1,0:T(8,128)}) custom-call(f32[16,2,128,1024]{3,2,1,0:T(8,128)} %all-gather.11.cloned.1.call-done.refs_0_), custom_call_target="tpu_custom_call" | custom-call | flops 10000000 | bytes 33554432 | tf_op jit(solution)/shard_map/pallas_call | solution.py:276
  728.5 0.0 all-gather.7.cloned.1.call-done.refs_0_
  728.5 13.9 %shard_map.132 = (f32[4096,1024]{1,0:T(8,128)}, f32[1024,4096]{1,0:T(8,128)}) custom-call(f32[16,2,128,1024]{3,2,1,0:T(8,128)} %all-gather.7.cloned.1.call-done.refs_0_), custom_call_target="tpu_custom_call" | custom-call | flops 10000000 | bytes 33554432 | tf_op jit(solution)/shard_map/pallas_call | solution.py:276
  742.4 4.1 all-gather.9.cloned.1.call-done.refs_0_
  746.4 14.0 %shard_map.135 = (f32[4096,1024]{1,0:T(8,128)}, f32[1024,4096]{1,0:T(8,128)}) custom-call(f32[16,2,128,1024]{3,2,1,0:T(8,128)} %all-gather.9.cloned.1.call-done.refs_0_, f32[4096,1024]{1,0:T(8,128)} %get-tuple-element.60.refs_1_, f32[1024,4096]{1,0:T(8,128)} %get-tuple-element.61.refs_2_), custom_call_target="tpu_custom_call", output_to_operand_aliasing={{0}: (1, {}), {1}: (2, {})} | custom-call | flops 10000000 | bytes 33554432 | tf_op jit(solution)/shard_map/pallas_call | solution.py:276
  760.4 64.6 %all-gather.5.cloned.1.call-done.refs_0_ = f32[16,2,128,1024]{3,2,1,0:T(8,128)} async-done(((f32[1,2,128,1024]{3,2,1,0:T(8,128)}), f32[16,2,128,1024]{3,2,1,0:T(8,128)}) %all-gather.5.cloned.1.call-update) | async-done | bytes 16777232 | tf_op jit(solution)/shard_map/all_gather | solution.py:302
  825.0 13.8 %shard_map.133 = (f32[4096,1024]{1,0:T(8,128)}, f32[1024,4096]{1,0:T(8,128)}) custom-call(f32[16,2,128,1024]{3,2,1,0:T(8,128)} %all-gather.5.cloned.1.call-done.refs_0_, f32[4096,1024]{1,0:T(8,128)} %get-tuple-element.54.refs_1_, f32[1024,4096]{1,0:T(8,128)} %get-tuple-element.55.refs_2_), custom_call_target="tpu_custom_call", output_to_operand_aliasing={{0}: (1, {}), {1}: (2, {})} | custom-call | flops 10000000 | bytes 33554432 | tf_op jit(solution)/shard_map/pallas_call | solution.py:276
Async XLA Ops:
  7.2 707.5 %all-gather.11.cloned.1.call-start = ((), (), s32[]{:S(2)}) async-start(), calls=%async_computation.3 | async-start | bytes 17825792 | tf_op jit(solution)/shard_map/all_gather | solution.py:302
  13.7 24.4 %copy-start = (bf16[2048,1024]{1,0:T(8,128)(2,1)S(1)}, bf16[2048,1024]{1,0:T(8,128)(2,1)}, u32[]{:S(2)}) copy-start(bf16[2048,1024]{1,0:T(8,128)(2,1)} %param.8) | copy-start | bytes 12582916
  13.7 24.4 %copy-start.3 = (bf16[1024,4096]{1,0:T(8,128)(2,1)S(1)}, bf16[1024,4096]{1,0:T(8,128)(2,1)}, u32[]{:S(2)}) copy-start(bf16[1024,4096]{1,0:T(8,128)(2,1)} %param.12) | copy-start | bytes 25165828
  90.2 24.9 %copy-start.1 = (bf16[2048,1024]{0,1:T(8,128)(2,1)S(1)}, bf16[2048,1024]{0,1:T(8,128)(2,1)}, u32[]{:S(2)}) copy-start(bf16[2048,1024]{0,1:T(8,128)(2,1)} %copy.28) | copy-start | bytes 12582916
  332.5 396.0 %all-gather.7.cloned.1.call-start = ((), (), s32[]{:S(2)}) async-start(), calls=%async_computation.1 | async-start | bytes 17825792 | tf_op jit(solution)/shard_map/all_gather | solution.py:302
  332.5 25.5 %copy-start.2 = (bf16[1024,4096]{1,0:T(8,128)(2,1)S(1)}, bf16[1024,4096]{1,0:T(8,128)(2,1)}, u32[]{:S(2)}) copy-start(bf16[1024,4096]{1,0:T(8,128)(2,1)} %param.14) | copy-start | bytes 25165828
  332.6 25.5 %copy-start.5 = (bf16[2048,1024]{1,0:T(8,128)(2,1)S(1)}, bf16[2048,1024]{1,0:T(8,128)(2,1)}, u32[]{:S(2)}) copy-start(bf16[2048,1024]{1,0:T(8,128)(2,1)} %refs_2_.3) | copy-start | bytes 12582916
  551.6 194.8 %all-gather.9.cloned.1.call-start = ((), (), s32[]{:S(2)}) async-start(), calls=%async_computation.2 | async-start | bytes 17825792 | tf_op jit(solution)/shard_map/all_gather | solution.py:302
  552.3 272.7 %all-gather.5.cloned.1.call-start = ((), (), s32[]{:S(2)}) async-start(), calls=%async_computation | async-start | bytes 17825792 | tf_op jit(solution)/shard_map/all_gather | solution.py:302
  668.9 24.3 %copy-start.4 = (bf16[1024,4096]{1,0:T(8,128)(2,1)S(1)}, bf16[1024,4096]{1,0:T(8,128)(2,1)}, u32[]{:S(2)}) copy-start(bf16[1024,4096]{1,0:T(8,128)(2,1)} %param.12) | copy-start | bytes 25165828
  668.9 24.2 %copy-start.6 = (bf16[2048,1024]{1,0:T(8,128)(2,1)S(1)}, bf16[2048,1024]{1,0:T(8,128)(2,1)}, u32[]{:S(2)}) copy-start(bf16[2048,1024]{1,0:T(8,128)(2,1)} %add_convert_fusion.3.refs_2_) | copy-start | bytes 12582916
Sparse Core Ops, SparseCore 0:
  332.6 75.5 all-gather.10
  551.7 116.2 all-gather.6
  670.3 76.1 all-gather.8
  748.5 76.4 all-gather.4

commit v2 on v0

v2 whole, which is shorter than its diff:
```python
import functools

import jax
import jax.numpy as jnp
from jax import lax
from jax.experimental import pallas as pl
from jax.experimental.pallas import tpu as pltpu
from jax.sharding import PartitionSpec as P


GELU_C = 0.7978845608028654
GELU_A = 0.044715
AXES = ("dz", "dy", "dx")
CHUNK = 256
QUARTER = 4
ROW_BLOCK = 512
VMEM_LIMIT = 67_000_000
SHARD_ROWS = 64
XYZ, YZX, ZXY = (2, 1, 0), (1, 0, 2), (0, 2, 1)
PIECES = (
    (0, 0, 40, 0, 1024, XYZ),
    (1, 0, 24, 0, 1024, YZX),
    (1, 24, 40, 0, 1024, ZXY),
    (0, 48, 16, 0, 1024, YZX),
    (0, 40, 8, 0, 512, XYZ),
    (0, 40, 8, 512, 512, YZX),
)
COUNT = len(PIECES)


def gelu_value(pre_act):
    pre_f = pre_act.astype(jnp.float32)
    return 0.5 * pre_f * (1.0 + jnp.tanh(GELU_C * (pre_f + GELU_A * pre_f * pre_f * pre_f)))


def mat_tn(left_op, right_op):
    return lax.dot_general(left_op, right_op, (((0,), (0,)), ((), ())), preferred_element_type=jnp.float32)


def mat_nt(left_op, right_op):
    return lax.dot_general(left_op, right_op, (((1,), (1,)), ((), ())), preferred_element_type=jnp.float32)


MESH = pl.DeviceIdType.MESH


def place():
    dz, dy, dx = lax.axis_index("dz"), lax.axis_index("dy"), lax.axis_index("dx")
    core = lax.rem(dx, 2)
    peers = ({"dz": 1 - dz}, {"dy": 1 - dy}, {"dx": lax.rem(dx + 2, 4)})
    return core, (dz, dy, lax.div(dx, 2)), {"dx": dx + 1 - 2 * core}, peers


def meet():
    _, _, partner, peers = place()
    barrier = pltpu.get_barrier_semaphore()
    for device in (partner, *peers):
        pl.semaphore_signal(barrier, inc=1, device_id=device, device_id_type=MESH)
    pl.semaphore_wait(barrier, 4)


class Early:
    scratch = [
        *[pltpu.VMEM((*lead, piece[2], piece[4]), jnp.float32) for lead in ((2, 2, 2), (2, 2, 2), (2, 2)) for piece in PIECES],
        pltpu.SemaphoreType.DMA((COUNT,)),
        pltpu.SemaphoreType.DMA((2 * COUNT,)),
        pltpu.SemaphoreType.DMA((2 * COUNT,)),
    ]

    def __init__(self, arrays, state, scratch):
        self.arrays, self.state = arrays, state
        self.acc, self.core_in, self.in_one = (scratch[at * COUNT:(at + 1) * COUNT] for at in range(3))
        self.own_sem, self.send_sem, self.recv_sem = scratch[3 * COUNT:]
        self.core, self.bits, self.partner, self.peers = place()

    def blocks(self, core):
        for piece, (array, row, rows, col, cols, order) in enumerate(PIECES):
            for index in range(8):
                zyx = (index // 4, (index // 2) % 2, index % 2)
                source = self.arrays[array].at[(index * 2) + core, pl.ds(row, rows), pl.ds(col, cols)]
                yield piece, source, tuple(zyx[axis] for axis in order)

    def begin(self):
        for piece, source, position in self.blocks(1 - self.core):
            pltpu.make_async_remote_copy(
                src_ref=source, dst_ref=self.core_in[piece].at[position],
                send_sem=self.send_sem.at[piece], recv_sem=self.recv_sem.at[piece],
                device_id=self.partner, device_id_type=MESH).start()
        for piece, source, position in self.blocks(self.core):
            pltpu.make_async_copy(source, self.acc[piece].at[position], self.own_sem.at[piece]).start()

    def axis_copy(self, piece):
        axis = PIECES[piece][-1][0]
        return pltpu.make_async_remote_copy(
            src_ref=self.acc[piece].at[1 - self.bits[axis]], dst_ref=self.in_one[piece],
            send_sem=self.send_sem.at[COUNT + piece], recv_sem=self.recv_sem.at[COUNT + piece],
            device_id=self.peers[axis], device_id_type=MESH)

    def turn(self):
        for piece in range(COUNT):
            whole = pltpu.make_async_remote_copy(
                src_ref=self.acc[piece], dst_ref=self.core_in[piece], send_sem=self.send_sem.at[piece],
                recv_sem=self.recv_sem.at[piece], device_id=self.partner, device_id_type=MESH)
            whole.wait_recv()
            whole.wait_send()
            pltpu.make_async_copy(self.acc[piece], self.acc[piece], self.own_sem.at[piece]).wait()

            @pl.loop(0, 4)
            def _(index, piece=piece):
                a, b = lax.div(index, 2), lax.rem(index, 2)
                self.acc[piece][a, b] = self.acc[piece][a, b] + self.core_in[piece][a, b]

            self.axis_copy(piece).start()

    def finish(self):
        for piece in range(COUNT):
            self.axis_copy(piece).wait()
            a = self.bits[PIECES[piece][-1][0]]
            for b in range(2):
                self.state[piece][b] = self.acc[piece][a, b] + self.in_one[piece][b]


class Late:
    scratch = [
        *[pltpu.VMEM((*lead, piece[2], piece[4]), jnp.float32) for lead in ((2,), (2,), ()) for piece in PIECES],
        pltpu.SemaphoreType.DMA((2 * COUNT,)),
        pltpu.SemaphoreType.DMA((2 * COUNT,)),
    ]

    def __init__(self, state, shard, scratch):
        self.state, self.shard = state, shard
        self.keep, self.in_two, self.in_three = (scratch[at * COUNT:(at + 1) * COUNT] for at in range(3))
        self.send_sem, self.recv_sem = scratch[3 * COUNT:]
        _, self.bits, _, self.peers = place()

    def axis_copy(self, phase, piece):
        axis = PIECES[piece][-1][1 + phase]
        source, target = ((self.state, self.in_two), (self.keep, self.in_three))[phase]
        slot = phase * COUNT + piece
        return pltpu.make_async_remote_copy(
            src_ref=source[piece].at[1 - self.bits[axis]], dst_ref=target[piece],
            send_sem=self.send_sem.at[slot], recv_sem=self.recv_sem.at[slot],
            device_id=self.peers[axis], device_id_type=MESH)

    def begin(self):
        for piece in range(COUNT):
            self.axis_copy(0, piece).start()

    def turn(self):
        for piece in range(COUNT):
            self.axis_copy(0, piece).wait()
            b = self.bits[PIECES[piece][-1][1]]
            self.keep[piece][...] = self.state[piece][b] + self.in_two[piece][...]
            self.axis_copy(1, piece).start()

    def finish(self):
        for piece, (array, row, rows, col, cols, order) in enumerate(PIECES):
            self.axis_copy(1, piece).wait()
            total = (self.keep[piece][self.bits[order[2]]] + self.in_three[piece][...]) * (1.0 / 16.0)
            self.shard[0, array, row:row + rows, col:col + cols] = total


STATE = [jax.ShapeDtypeStruct((2, 2, piece[2], piece[4]), jnp.float32) for piece in PIECES]


def run_at(step, half, work):
    for slot, actions in work.items():
        if slot % 2 == half:
            @pl.when(step == slot // 2)
            def _(actions=actions):
                for action in actions:
                    action()


SHARD = jax.ShapeDtypeStruct((1, 2, SHARD_ROWS, 1024), jnp.float32)
IN_VMEM = pl.BlockSpec(memory_space=pltpu.VMEM)
GROUPS = (1, 1, 1, 1, 1, 1, 2)
ANY = pl.BlockSpec(memory_space=pl.ANY)
RESIDENT = pl.Buffered(1)


def activation_and_slope(pre):
    square = pre * pre
    half = 0.5 + 0.5 * jnp.tanh(pre * (GELU_C + (GELU_C * GELU_A) * square))
    slope = half + pre * (half * (1.0 - half)) * (2.0 * GELU_C + (6.0 * GELU_C * GELU_A) * square)
    return (pre * half).astype(jnp.bfloat16), slope


def stage_kernel(early, late, fused, passed, *refs):
    (in_one, in_two, g_one, g_two, w_ref), refs = refs[:5], refs[5:]
    if fused:
        w_pre, refs = refs[0], refs[1:]
    else:
        (p_one, p_two), refs = refs[:2], refs[2:]
    if early:
        arrays, refs = refs[:2], refs[2:]
    if late:
        state_in, refs = refs[:COUNT], refs[COUNT:]
    if passed:
        refs = refs[2:]
    (dz_one, dz_two, ua, ub), refs = refs[:4], refs[4:]
    if early:
        state_out, refs = refs[:COUNT], refs[COUNT:]
    if late:
        shard, refs = refs[0], refs[1:]
    act, refs = refs[0], refs[1:]
    step = pl.program_id(0)
    work, ends = {}, []
    if early:
        first = Early(arrays, state_out, refs[:len(Early.scratch)])
        work = {0: [meet, first.begin], 2: [first.turn]}
        ends = [first.finish]
    if late:
        second = Late(state_in, shard, refs[len(Early.scratch):])
        work[0].append(second.begin)
        work[4] = [second.turn]
        ends.append(second.finish)
    block = ROW_BLOCK if fused else 2 * ROW_BLOCK
    per_mb = in_one.shape[0] // block

    def block_of(number):
        mb, row = divmod(number, per_mb)
        return mb, pl.ds(row * block, block), (in_one, in_two)[mb], (g_one, g_two)[mb], (dz_one, dz_two)[mb]

    def front(number):
        mb, rows, in_ref, g_ref, _ = block_of(number)
        upstream = mat_nt(g_ref[rows, :], w_ref[...])
        if fused:
            return upstream, jnp.dot(in_ref[rows, :], w_pre[...], preferred_element_type=jnp.float32)
        return upstream, (p_one, p_two)[mb][rows, :]

    def back(number):
        _, rows, in_ref, g_ref, dz_ref = block_of(number)
        from_act = mat_tn(act[rows, :], g_ref[rows, :]).reshape(ua.shape)
        from_dz = mat_tn(dz_ref[rows, :], in_ref[rows, :]).reshape(ub.shape)
        if number == 0:
            ua[...] = from_act
            ub[...] = from_dz
        else:
            ua[...] += from_act
            ub[...] += from_dz

    run_at(step, 0, work)
    ready = front(0)
    for number in range(2 * per_mb):
        upstream, pre = ready
        if number + 1 < 2 * per_mb:
            ready = front(number + 1)
        _, rows, _, _, dz_ref = block_of(number)
        act[rows, :], slope = activation_and_slope(pre.astype(jnp.bfloat16).astype(jnp.float32))
        dz_ref[rows, :] = (upstream * slope).astype(jnp.bfloat16)
        if number:
            back(number - 1)
    back(2 * per_mb - 1)
    for action in ends:
        pl.when(step == QUARTER - 1)(action)


def stage(quarter, ins, grads, weight, w_pre=None, pres=None, passed=None, ride=None):
    rows = ins[0].shape[0]
    hidden = weight.shape[0]
    base = quarter * QUARTER
    column = pl.BlockSpec((rows, CHUNK), lambda c: (0, base + c))
    whole = pl.BlockSpec((rows, 1024), lambda c: (0, 0), pipeline_mode=RESIDENT)
    operands = [*ins, *grads, weight]
    in_specs = [whole] * 4 + [pl.BlockSpec((CHUNK, 1024), lambda c: (base + c, 0))]
    if w_pre is not None:
        operands.append(w_pre)
        in_specs.append(pl.BlockSpec((1024, CHUNK), lambda c: (0, base + c)))
    else:
        operands += list(pres)
        in_specs += [column, column]
    unit_shape = jax.ShapeDtypeStruct((16, SHARD_ROWS, 1024), jnp.float32)
    unit_spec = pl.BlockSpec((CHUNK // SHARD_ROWS, SHARD_ROWS, 1024), lambda c: (c, 0, 0))
    out_shape = [jax.ShapeDtypeStruct((rows, hidden), jnp.bfloat16)] * 2 + [unit_shape] * 2
    out_specs = [column, column, unit_spec, unit_spec]
    scratch = [pltpu.VMEM((rows, CHUNK), jnp.bfloat16)]
    params = dict(vmem_limit_bytes=VMEM_LIMIT, dimension_semantics=("arbitrary",))
    unit, state, collective_id = ride
    if unit is not None:
        operands += list(unit)
        in_specs += [ANY, ANY]
        out_shape += STATE
        out_specs += [IN_VMEM] * COUNT
        scratch += Early.scratch
        params.update(collective_id=collective_id, has_side_effects=True)
    if state is not None:
        operands += list(state)
        in_specs += [IN_VMEM] * COUNT
        out_shape.append(SHARD)
        out_specs.append(IN_VMEM)
        scratch += Late.scratch
    aliases = {}
    if passed is not None:
        aliases = {len(operands): 0, len(operands) + 1: 1}
        operands += list(passed)
        in_specs += [ANY, ANY]
    dots = 4 if w_pre is not None else 3
    out = pl.pallas_call(
        functools.partial(stage_kernel, unit is not None, state is not None, w_pre is not None, passed is not None),
        grid=(QUARTER,),
        out_shape=out_shape,
        in_specs=in_specs,
        out_specs=out_specs,
        scratch_shapes=scratch,
        input_output_aliases=aliases,
        compiler_params=pltpu.CompilerParams(**params),
        cost_estimate=pl.CostEstimate(
            flops=2 * dots * 2 * rows * 1024 * CHUNK * QUARTER, bytes_accessed=48 << 20, transcendentals=0),
    )(*operands)
    half_done = out[4:4 + COUNT] if unit is not None else None
    return (out[0], out[1]), (out[2], out[3]), half_done, (out[-1] if state is not None else None)


DX_ROWS = 512


def last_kernel(early, *refs):
    (dz_ref, add_ref, w_ref), refs = refs[:3], refs[3:]
    if early:
        arrays, refs = refs[:2], refs[2:]
    state_in, dx_ref, refs = refs[:COUNT], refs[COUNT], refs[COUNT + 1:]
    if early:
        state_out, refs = refs[:COUNT], refs[COUNT:]
    shard, refs = refs[0], refs[1:]
    step = pl.program_id(0)
    second = Late(state_in, shard, refs[:len(Late.scratch)])
    work, ends = {0: [meet], 4: []}, []
    if early:
        first = Early(arrays, state_out, refs[len(Late.scratch):])
        work[0].append(first.begin)
        work[4].append(first.turn)
        ends.append(first.finish)
    work[0].append(second.begin)
    work[4].append(second.turn)
    ends.append(second.finish)
    run_at(step, 0, work)
    dx_ref[...] = (mat_nt(dz_ref[...], w_ref[...]) + add_ref[...].astype(jnp.float32)).astype(jnp.bfloat16)
    for action in ends:
        pl.when(step == pl.num_programs(0) - 1)(action)


def last_stage(dz, add, weight, unit, state, collective_id):
    rows, hidden = dz.shape
    wide = pl.BlockSpec((DX_ROWS, hidden), lambda r: (r, 0))
    narrow = pl.BlockSpec((DX_ROWS, 1024), lambda r: (r, 0))
    weight_spec = pl.BlockSpec((1024, hidden), lambda r: (0, 0), pipeline_mode=RESIDENT)
    early = unit is not None
    out = pl.pallas_call(
        functools.partial(last_kernel, early),
        grid=(rows // DX_ROWS,),
        out_shape=[jax.ShapeDtypeStruct((rows, 1024), jnp.bfloat16), *(STATE if early else []), SHARD],
        in_specs=[wide, narrow, weight_spec, *([ANY, ANY] if early else []), *[IN_VMEM] * COUNT],
        out_specs=[narrow, *([IN_VMEM] * COUNT if early else []), IN_VMEM],
        scratch_shapes=[*Late.scratch, *(Early.scratch if early else [])],
        compiler_params=pltpu.CompilerParams(
            collective_id=collective_id, has_side_effects=True, vmem_limit_bytes=VMEM_LIMIT,
            dimension_semantics=("arbitrary",)),
        cost_estimate=pl.CostEstimate(flops=2 * rows * 1024 * hidden, bytes_accessed=32 << 20, transcendentals=0),
    )(dz, add, weight, *(unit if early else ()), *state)
    return out[0], out[1:1 + COUNT] if early else None, out[-1]


FORWARD_CHUNK = 512


def forward_kernel(x_ref, w_one, w_two, pre_ref, mid_ref, acc):
    step = pl.program_id(0)
    count = x_ref.shape[0] // ROW_BLOCK

    @pl.when(step == 0)
    def _():
        acc[...] = x_ref[...].astype(jnp.float32)

    def front(number):
        return jnp.dot(x_ref[pl.ds(number * ROW_BLOCK, ROW_BLOCK), :], w_one[...], preferred_element_type=jnp.float32)

    ready = front(0)
    for number in range(count):
        rows = pl.ds(number * ROW_BLOCK, ROW_BLOCK)
        pre = ready.astype(jnp.bfloat16)
        if number + 1 < count:
            ready = front(number + 1)
        pre_ref[rows, :] = pre
        act = gelu_value(pre).astype(jnp.bfloat16)
        acc[rows, :] += jnp.dot(act, w_two[...], preferred_element_type=jnp.float32)

    @pl.when(step == pl.num_programs(0) - 1)
    def _():
        mid_ref[...] = acc[...].astype(jnp.bfloat16)


def forward(x_rows, w_one, w_two):
    rows, hidden = x_rows.shape[0], w_one.shape[1]
    return pl.pallas_call(
        forward_kernel,
        grid=(hidden // FORWARD_CHUNK,),
        out_shape=[jax.ShapeDtypeStruct((rows, hidden), jnp.bfloat16), jax.ShapeDtypeStruct((rows, 1024), jnp.bfloat16)],
        in_specs=[
            pl.BlockSpec((rows, 1024), lambda c: (0, 0), pipeline_mode=RESIDENT),
            pl.BlockSpec((1024, FORWARD_CHUNK), lambda c: (0, c)),
            pl.BlockSpec((FORWARD_CHUNK, 1024), lambda c: (c, 0)),
        ],
        out_specs=[pl.BlockSpec((rows, FORWARD_CHUNK), lambda c: (0, c)), pl.BlockSpec((rows, 1024), lambda c: (0, 0))],
        scratch_shapes=[pltpu.VMEM((rows, 1024), jnp.float32)],
        compiler_params=pltpu.CompilerParams(vmem_limit_bytes=VMEM_LIMIT, dimension_semantics=("arbitrary",)),
        cost_estimate=pl.CostEstimate(flops=4 * rows * 1024 * hidden, bytes_accessed=40 << 20, transcendentals=0),
    )(x_rows, w_one, w_two)


def assemble_kernel(*refs):
    source, (row_type, col_type) = refs[0], refs[-2:]
    row_type[...] = source[:, 0, 0].reshape(row_type.shape)
    col_type[...] = source[:, 0, 1].reshape(row_type.shape).T


def copy_kernel(one, two, out_one, out_two):
    out_one[...] = one[...]
    out_two[...] = two[...]


def own_buffers(one, two):
    spec = pl.BlockSpec((512, 1024), lambda r: (r, 0))
    return pl.pallas_call(
        copy_kernel,
        grid=(one.shape[0] // 512,),
        out_shape=[jax.ShapeDtypeStruct(one.shape, one.dtype)] * 2,
        in_specs=[spec, spec],
        out_specs=[spec, spec],
        cost_estimate=pl.CostEstimate(flops=10_000_000, bytes_accessed=16 << 20, transcendentals=0),
    )(one, two)


def assemble(quarter, gathered, member, before=None):
    base = quarter * QUARTER
    operands = [gathered]
    in_specs = [pl.BlockSpec((CHUNK // SHARD_ROWS, 1, 2, SHARD_ROWS, 1024), lambda c: (c, member, 0, 0, 0))]
    aliases = {}
    if before is not None:
        operands += list(before)
        in_specs += [ANY, ANY]
        aliases = {1: 0, 2: 1}
    return pl.pallas_call(
        assemble_kernel,
        grid=(QUARTER,),
        out_shape=[jax.ShapeDtypeStruct((4096, 1024), jnp.float32), jax.ShapeDtypeStruct((1024, 4096), jnp.float32)],
        in_specs=in_specs,
        out_specs=[pl.BlockSpec((CHUNK, 1024), lambda c: (base + c, 0)), pl.BlockSpec((1024, CHUNK), lambda c: (0, base + c))],
        input_output_aliases=aliases,
        cost_estimate=pl.CostEstimate(flops=10_000_000, bytes_accessed=16 << 20, transcendentals=0),
    )(*operands)


def solution(mesh):
    row_spec = P(AXES, None)
    rep_spec = P(None, None)

    def through(dz_rows, weight, grad_rows):
        return (mat_nt(dz_rows, weight) + grad_rows.astype(jnp.float32)).astype(jnp.bfloat16)

    def gather(shards):
        whole = lax.all_gather(jnp.stack(shards, axis=1), AXES, axis=0, tiled=True)
        return [(whole, member) for member in range(len(shards))]

    def whole_step(x_one, g_one, x_two, g_two, w_one, w_two, w_three, w_four):
        pres_and_mids = (forward(x_one, w_one, w_two), forward(x_two, w_one, w_two))
        pres = tuple(pair[0] for pair in pres_and_mids)
        mids = tuple(pair[1] for pair in pres_and_mids)
        wholes, waiting = [], []
        unit = state = None
        rides = groups = 0

        def collect(shard):
            nonlocal groups
            waiting.append(shard)
            if len(waiting) == GROUPS[groups]:
                wholes.extend(gather(waiting))
                waiting.clear()
                groups += 1

        def quarter_of(quarter, *operands, **named):
            nonlocal unit, state, rides
            rides += unit is not None
            ride = (unit, state, rides)
            dzs, unit, state, shard = stage(quarter, *operands, ride=ride, **named)
            if shard is not None:
                collect(shard)
            return dzs

        dz_three = None
        for quarter in range(4):
            dz_three = quarter_of(quarter, mids, (g_one, g_two), w_four, w_pre=w_three, passed=dz_three)
        dmid = (through(dz_three[0], w_three, g_one), through(dz_three[1], w_three, g_two))
        dz_one = None
        for quarter in range(4):
            dz_one = quarter_of(quarter, (x_one, x_two), dmid, w_two, pres=pres, passed=dz_one)
        dx_one, state, shard = last_stage(dz_one[0], dmid[0], w_one, unit, state, 8)
        collect(shard)
        dx_two, _, shard = last_stage(dz_one[1], dmid[1], w_one, None, state, 9)
        collect(shard)
        dx_one, dx_two = own_buffers(dx_one, dx_two)
        upper = lower = None
        for quarter in range(4):
            upper = assemble(quarter, *wholes[quarter], upper)
        for quarter in range(4):
            if quarter == 3:
                lower, upper, dx_one, dx_two = lax.optimization_barrier((lower, upper, dx_one, dx_two))
            lower = assemble(quarter, *wholes[4 + quarter], lower)
        return lower[1], lower[0], upper[1], upper[0], dx_one, dx_two

    return jax.shard_map(
        whole_step,
        mesh=mesh,
        in_specs=(row_spec, row_spec, row_spec, row_spec, rep_spec, rep_spec, rep_spec, rep_spec),
        out_specs=(rep_spec, rep_spec, rep_spec, rep_spec, row_spec, row_spec),
        check_vma=False,
    )
```

time: 1970 us -> 889 us (0.45)
  waiting for transfers between devices: 1250 us -> 170 us
  Pallas kernels: 0 us -> 646 us
  matrix products: 630 us -> 48.4 us
  local copies, waits for them, and re-layouts: 49.2 us -> 0.01 us
    pallas_call x0 -> x21, Pallas kernels: none -> 646 us  [the longest x8 403 us: stage(): pl.pallas_call(functools.partial(stage_kernel, unit is not None, state is...]
    all_gather x12 -> x7, waiting for transfers between devices: 733 us -> 168 us  [gather(): whole = lax.all_gather(jnp.stack(shards, axis=1), AXES, axis=0, tiled=True)]
    reduce_scatter x12 -> x0, waiting for transfers between devices: 520 us -> none  [the longest x4 215 us: mean_over_devices(): lax.psum_scatter(shard_sum, 'dy', scatter_dimension=0, tiled=True)]
    dot_general x14 -> x0, matrix products: 366 us -> none  [the longest x8 227 us: mat_tn(): lax.dot_general(left_op, right_op, (((0,), (0,)), ((), ())), preferred_el...]
    dot_general x8 -> x2, matrix products: 264 us -> 48.4 us  [mat_nt(): lax.dot_general(left_op, right_op, (((1,), (1,)), ((), ())), preferred_el...]
    unnamed x59 -> x2, local copies, waits for them, and re-layouts: 49.2 us -> 0.01 us
  transfers between devices with their start and end apart: 24 -> 7, of which waited for: 22 -> 4; matrix products, arithmetic and copies ran while one was open for 23% -> 6% of each run, Pallas kernels for 0% -> 43%
where the time goes in v2:
time: 889 us; the launch traced here: 882 us
  Pallas kernels  646 us (73%)
  waiting for transfers between devices  170 us (19%)
  matrix products  48.4 us (5%)
  between operations  14.4 us (2%)
    pallas_call x8, Pallas kernels, stage(): pl.pallas_call(functools.partial(stage_kernel, unit is not None, state is...  403 us
    all_gather x7, waiting for transfers between devices, gather(): whole = lax.all_gather(jnp.stack(shards, axis=1), AXES, axis=0, tiled=True)  168 us
    pallas_call x2, Pallas kernels, forward(): pl.pallas_call(forward_kernel, grid=(hidden // FORWARD_CHUNK,), out_shape...  91.5 us
    pallas_call x2, Pallas kernels, last_stage(): pl.pallas_call(functools.partial(last_kernel, early), grid=(rows // DX_RO...  83.7 us
    pallas_call x8, Pallas kernels, assemble(): pl.pallas_call(assemble_kernel, grid=(QUARTER,), out_shape=[jax.ShapeDtyp...  60.4 us
    dot_general x2, matrix products, mat_nt(): lax.dot_general(left_op, right_op, (((1,), (1,)), ((), ())), preferred_el...  48.4 us
  transfers between devices with their start and end apart: 7, of which 4 were waited for; matrix products, arithmetic and copies ran while one was open for 6% of the time, Pallas kernels for 43%

profile of v2, /device:TPU:0, one launch (start us, length us, event | category | flops | bytes accessed | tf_op | source)
XLA Modules:
  0.0 881.7 jit_solution(6004956210586556790)
XLA Ops:
  7.2 0.0 all-gather.26.cloned.1.call-start
  7.2 45.8 %shard_map.127 = (bf16[2048,4096]{1,0:T(8,128)(2,1)}, bf16[2048,1024]{1,0:T(8,128)(2,1)}) custom-call(bf16[2048,1024]{1,0:T(8,128)(2,1)} %refs_0_.7, bf16[1024,4096]{1,0:T(8,128)(2,1)} %refs_2_.11, bf16[4096,1024]{1,0:T(8,128)(2,1)} %refs_4_.15), custom_call_target="tpu_custom_call" | custom-call | flops 34359738368 | bytes 41943040 | tf_op jit(solution)/shard_map/pallas_call | solution.py:395
  53.0 45.8 %shard_map.128 = (bf16[2048,4096]{1,0:T(8,128)(2,1)}, bf16[2048,1024]{1,0:T(8,128)(2,1)}) custom-call(bf16[2048,1024]{1,0:T(8,128)(2,1)} %refs_1_.7, bf16[1024,4096]{1,0:T(8,128)(2,1)} %refs_2_.11, bf16[4096,1024]{1,0:T(8,128)(2,1)} %refs_4_.15), custom_call_target="tpu_custom_call" | custom-call | flops 34359738368 | bytes 41943040 | tf_op jit(solution)/shard_map/pallas_call | solution.py:395
  98.8 49.0 %shard_map.129 = (bf16[2048,4096]{1,0:T(8,128)(2,1)}, bf16[2048,4096]{1,0:T(8,128)(2,1)}, f32[16,64,1024]{2,1,0:T(8,128)}, f32[16,64,1024]{2,1,0:T(8,128)}) custom-call(bf16[2048,1024]{1,0:T(8,128)(2,1)} %get-tuple-element.124.refs_0_, bf16[2048,1024]{1,0:T(8,128)(2,1)} %get-tuple-element.125.refs_1_, bf16[2048,1024]{1,0:T(8,128)(2,1)} %refs_2_.9, ...), custom_call_target="tpu_custom_call" | custom-call | flops 34359738368 | bytes 50331648 | tf_op jit(solution)/shard_map/pallas_call | solution.py:299
  147.7 55.2 %shard_map.130 = (bf16[2048,4096]{1,0:T(8,128)(2,1)}, bf16[2048,4096]{1,0:T(8,128)(2,1)}, f32[16,64,1024]{2,1,0:T(8,128)}, f32[16,64,1024]{2,1,0:T(8,128)}, f32[...) custom-call(bf16[2048,1024]{1,0:T(8,128)(2,1)} %get-tuple-element.12, ...), custom_call_target="tpu_custom_call", output_to_operand_aliasing={{0}: (8, {}), {1}: (9, {})} | custom-call | flops 34359738368 | bytes 50331648 | tf_op jit(solution)/shard_map/pallas_call | solution.py:299
  203.0 54.7 %shard_map.131 = (bf16[2048,4096]{1,0:T(8,128)(2,1)}, bf16[2048,4096]{1,0:T(8,128)(2,1)}, f32[16,64,1024]{2,1,0:T(8,128)}, f32[16,64,1024]{2,1,0:T(8,128)}, f32[...) custom-call(bf16[2048,1024]{1,0:T(8,128)(2,1)} %get-tuple-element.12, ...), custom_call_target="tpu_custom_call", output_to_operand_aliasing={{0}: (14, {}), {1}: (15, {})} | custom-call | flops 34359738368 | bytes 50331648 | tf_op jit(solution)/shard_map/pallas_call | solution.py:299
  257.7 0.0 all-gather.26.cloned.1.call-update
  257.8 0.0 all-gather.18.cloned.1.call-start
  257.8 56.2 %shard_map.132 = (bf16[2048,4096]{1,0:T(8,128)(2,1)}, bf16[2048,4096]{1,0:T(8,128)(2,1)}, f32[16,64,1024]{2,1,0:T(8,128)}, f32[16,64,1024]{2,1,0:T(8,128)}, f32[...) custom-call(bf16[2048,1024]{1,0:T(8,128)(2,1)} %get-tuple-element.12, ...), custom_call_target="tpu_custom_call", output_to_operand_aliasing={{0}: (14, {}), {1}: (15, {})} | custom-call | flops 34359738368 | bytes 50331648 | tf_op jit(solution)/shard_map/pallas_call | solution.py:299
  314.0 0.0 copy-start
  314.0 24.6 %add_convert_fusion.refs_3_.refs_1_ = bf16[2048,1024]{1,0:T(8,128)(2,1)} fusion(bf16[2048,1024]{1,0:T(8,128)(2,1)} %refs_3_.7, bf16[2048,4096]{1,0:T(8,128)(2,1)} %get-tuple-element.151, bf16[1024,4096]{1,0:T(8,128)(2,1)} %refs_5_.7), kind=kOutput, calls=%fused_computation | convolution fusion | flops 17186160640 | bytes 33554432 | tf_op jit(solution)/shard_map/dot_general | solution.py:41
  338.7 0.0 copy-done
  338.7 23.8 %add_convert_fusion.1.refs_2_.refs_1_ = bf16[2048,1024]{1,0:T(8,128)(2,1)} fusion(bf16[2048,1024]{1,0:T(8,128)(2,1)S(1)} %copy-done, bf16[2048,4096]{1,0:T(8,128)(2,1)} %get-tuple-element.150, bf16[1024,4096]{1,0:T(8,128)(2,1)} %refs_5_.7), kind=kOutput, calls=%fused_computation.1 | convolution fusion | flops 17186160640 | bytes 33554432 | tf_op jit(solution)/shard_map/dot_general | solution.py:41
  362.5 44.4 %shard_map.133 = (bf16[2048,4096]{1,0:T(8,128)(2,1)}, bf16[2048,4096]{1,0:T(8,128)(2,1)}, f32[16,64,1024]{2,1,0:T(8,128)}, f32[16,64,1024]{2,1,0:T(8,128)}, f32[...) custom-call(bf16[2048,1024]{1,0:T(8,128)(2,1)} %refs_0_.7, ...), custom_call_target="tpu_custom_call" | custom-call | flops 25769803776 | bytes 50331648 | tf_op jit(solution)/shard_map/pallas_call | solution.py:299
  406.9 43.6 %shard_map.134 = (bf16[2048,4096]{1,0:T(8,128)(2,1)}, bf16[2048,4096]{1,0:T(8,128)(2,1)}, f32[16,64,1024]{2,1,0:T(8,128)}, f32[16,64,1024]{2,1,0:T(8,128)}, f32[...) custom-call(bf16[2048,1024]{1,0:T(8,128)(2,1)} %refs_0_.7, ...), custom_call_target="tpu_custom_call", output_to_operand_aliasing={{0}: (15, {}), {1}: (16, {})} | custom-call | flops 25769803776 | bytes 50331648 | tf_op jit(solution)/shard_map/pallas_call | solution.py:299
  450.5 44.7 %shard_map.135 = (bf16[2048,4096]{1,0:T(8,128)(2,1)}, bf16[2048,4096]{1,0:T(8,128)(2,1)}, f32[16,64,1024]{2,1,0:T(8,128)}, f32[16,64,1024]{2,1,0:T(8,128)}, f32[...) custom-call(bf16[2048,1024]{1,0:T(8,128)(2,1)} %refs_0_.7, ...), custom_call_target="tpu_custom_call", output_to_operand_aliasing={{0}: (15, {}), {1}: (16, {})} | custom-call | flops 25769803776 | bytes 50331648 | tf_op jit(solution)/shard_map/pallas_call | solution.py:299
  495.2 0.0 all-gather.18.cloned.1.call-update
  495.3 0.0 all-gather.24.cloned.1.call-start
  495.3 0.7 all-gather.24.cloned.1.call-update
  496.0 0.0 all-gather.22.cloned.1.call-start
  496.0 0.5 all-gather.22.cloned.1.call-update
  496.6 0.0 all-gather.20.cloned.1.call-start
  496.6 0.5 all-gather.20.cloned.1.call-update
  497.2 0.0 all-gather.16.cloned.1.call-start
  497.2 55.4 %shard_map.136 = (bf16[2048,4096]{1,0:T(8,128)(2,1)}, bf16[2048,4096]{1,0:T(8,128)(2,1)}, f32[16,64,1024]{2,1,0:T(8,128)}, f32[16,64,1024]{2,1,0:T(8,128)}, f32[...) custom-call(bf16[2048,1024]{1,0:T(8,128)(2,1)} %refs_0_.7, ...), custom_call_target="tpu_custom_call", output_to_operand_aliasing={{0}: (15, {}), {1}: (16, {})} | custom-call | flops 25769803776 | bytes 50331648 | tf_op jit(solution)/shard_map/pallas_call | solution.py:299
  552.6 0.0 all-gather.16.cloned.1.call-update
  552.6 0.0 all-gather.14.cloned.1.call-start
  552.7 50.5 %shard_map.137 = (bf16[2048,1024]{1,0:T(8,128)(2,1)}, f32[2,2,40,1024]{3,2,1,0:T(8,128)}, f32[2,2,24,1024]{3,2,1,0:T(8,128)}, f32[2,2,40,1024]{3,2,1,0:T(8,128)}...) custom-call(bf16[2048,4096]{1,0:T(8,128)(2,1)} %get-tuple-element.19, ...), custom_call_target="tpu_custom_call" | custom-call | flops 17179869184 | bytes 33554432 | tf_op jit(solution)/shard_map/pallas_call | solution.py:349
  603.2 33.2 %shard_map.138 = (bf16[2048,1024]{1,0:T(8,128)(2,1)}, f32[1,2,64,1024]{3,2,1,0:T(8,128)}) custom-call(bf16[2048,4096]{1,0:T(8,128)(2,1)} %get-tuple-element.202.refs_0_, bf16[2048,1024]{1,0:T(8,128)(2,1)} %add_convert_fusion.refs_3_.refs_1_, bf16[1024,4096]{1,0:T(8,128)(2,1)} %refs_2_.11, f32[2,2,40,1024]{3,2,1,0:T(8,128)} %get-tuple-element.203.refs_3_, ...), custom_call_target="tpu_custom_call" | custom-call | flops 17179869184 | bytes 33554432 | tf_op jit(solution)/shard_map/pallas_call | solution.py:349
  636.4 2.4 pad_maximum_fusion
  638.7 0.0 all-gather.14.cloned.1.call-update
  638.8 7.0 shard_map.146
  645.8 0.0 all-gather.26.cloned.1.call-done
  645.8 7.6 shard_map.142
  653.4 0.0 all-gather.18.cloned.1.call-done
  653.4 8.1 shard_map.139
  661.5 0.0 all-gather.24.cloned.1.call-done
  661.5 7.5 shard_map.143
  669.0 9.7 %all-gather.22.cloned.1.call-done = f32[16,2,64,1024]{3,2,1,0:T(8,128)} async-done(((f32[1,2,64,1024]{3,2,1,0:T(8,128)}), f32[16,2,64,1024]{3,2,1,0:T(8,128)}) %all-gather.22.cloned.1.call-update) | async-done | bytes 8388624 | tf_op jit(solution)/shard_map/all_gather | solution.py:462
  678.7 7.4 shard_map.144
  686.2 43.7 %all-gather.20.cloned.1.call-done = f32[16,2,64,1024]{3,2,1,0:T(8,128)} async-done(((f32[1,2,64,1024]{3,2,1,0:T(8,128)}), f32[16,2,64,1024]{3,2,1,0:T(8,128)}) %all-gather.20.cloned.1.call-update) | async-done | bytes 8388624 | tf_op jit(solution)/shard_map/all_gather | solution.py:462
  729.9 7.4 shard_map.145
  737.3 43.7 %all-gather.16.cloned.1.call-done = f32[16,2,64,1024]{3,2,1,0:T(8,128)} async-done(((f32[1,2,64,1024]{3,2,1,0:T(8,128)}), f32[16,2,64,1024]{3,2,1,0:T(8,128)}) %all-gather.16.cloned.1.call-update) | async-done | bytes 8388624 | tf_op jit(solution)/shard_map/all_gather | solution.py:462
  781.0 7.4 shard_map.140
  788.4 71.3 %all-gather.14.cloned.1.call-done.refs_0_ = f32[16,2,2,64,1024]{4,3,2,1,0:T(8,128)} async-done(((f32[1,2,2,64,1024]{4,3,2,1,0:T(8,128)}), f32[16,2,2,64,1024]{4,3,2,1,0:T(8,128)}) %all-gather.14.cloned.1.call-update) | async-done | bytes 16777232 | tf_op jit(solution)/shard_map/all_gather | solution.py:462
  859.7 7.4 shard_map.141
  867.2 7.4 shard_map.147
Async XLA Ops:
  7.2 638.6 %all-gather.26.cloned.1.call-start = ((), (), s32[]{:S(2)}) async-start(), calls=%async_computation.6 | async-start | bytes 8912896 | tf_op jit(solution)/shard_map/all_gather | solution.py:462
  257.8 395.6 %all-gather.18.cloned.1.call-start = ((), (), s32[]{:S(2)}) async-start(), calls=%async_computation.2 | async-start | bytes 8912896 | tf_op jit(solution)/shard_map/all_gather | solution.py:462
  314.0 24.6 %copy-start = (bf16[2048,1024]{1,0:T(8,128)(2,1)S(1)}, bf16[2048,1024]{1,0:T(8,128)(2,1)}, u32[]{:S(2)}) copy-start(bf16[2048,1024]{1,0:T(8,128)(2,1)} %refs_2_.9) | copy-start | bytes 12582916
  495.3 166.3 %all-gather.24.cloned.1.call-start = ((), (), s32[]{:S(2)}) async-start(), calls=%async_computation.5 | async-start | bytes 8912896 | tf_op jit(solution)/shard_map/all_gather | solution.py:462
  496.0 182.7 %all-gather.22.cloned.1.call-start = ((), (), s32[]{:S(2)}) async-start(), calls=%async_computation.4 | async-start | bytes 8912896 | tf_op jit(solution)/shard_map/all_gather | solution.py:462
  496.6 233.3 %all-gather.20.cloned.1.call-start = ((), (), s32[]{:S(2)}) async-start(), calls=%async_computation.3 | async-start | bytes 8912896 | tf_op jit(solution)/shard_map/all_gather | solution.py:462
  497.2 283.8 %all-gather.16.cloned.1.call-start = ((), (), s32[]{:S(2)}) async-start(), calls=%async_computation.1 | async-start | bytes 8912896 | tf_op jit(solution)/shard_map/all_gather | solution.py:462
  552.6 307.1 %all-gather.14.cloned.1.call-start = ((), (), s32[]{:S(2)}) async-start(), calls=%async_computation | async-start | bytes 17825792 | tf_op jit(solution)/shard_map/all_gather | solution.py:462
Sparse Core Ops, SparseCore 0:
  257.9 64.5 all-gather.25
  495.4 62.6 all-gather.17
  560.3 65.9 all-gather.23
  628.5 50.2 all-gather.21
  680.8 48.9 all-gather.19
  731.9 48.9 all-gather.15
  783.2 76.4 all-gather.13

commit v3 on v2

--- a/solution.py
+++ b/solution.py
@@ -256,7 +256,7 @@
         pl.when(step == QUARTER - 1)(action)
 
 
-def stage(quarter, ins, grads, weight, w_pre=None, pres=None, passed=None, ride=None):
+def stage(unit, state, quarter, ins, grads, weight, collective_id, w_pre=None, pres=None, passed=None):
     rows = ins[0].shape[0]
     hidden = weight.shape[0]
     base = quarter * QUARTER
@@ -276,7 +276,6 @@
     out_specs = [column, column, unit_spec, unit_spec]
     scratch = [pltpu.VMEM((rows, CHUNK), jnp.bfloat16)]
     params = dict(vmem_limit_bytes=VMEM_LIMIT, dimension_semantics=("arbitrary",))
-    unit, state, collective_id = ride
     if unit is not None:
         operands += list(unit)
         in_specs += [ANY, ANY]
@@ -340,7 +339,7 @@
         pl.when(step == pl.num_programs(0) - 1)(action)
 
 
-def last_stage(dz, add, weight, unit, state, collective_id):
+def last_stage(unit, state, dz, add, weight, collective_id):
     rows, hidden = dz.shape
     wide = pl.BlockSpec((DX_ROWS, hidden), lambda r: (r, 0))
     narrow = pl.BlockSpec((DX_ROWS, 1024), lambda r: (r, 0))
@@ -455,9 +454,6 @@
     row_spec = P(AXES, None)
     rep_spec = P(None, None)
 
-    def through(dz_rows, weight, grad_rows):
-        return (mat_nt(dz_rows, weight) + grad_rows.astype(jnp.float32)).astype(jnp.bfloat16)
-
     def gather(shards):
         whole = lax.all_gather(jnp.stack(shards, axis=1), AXES, axis=0, tiled=True)
         return [(whole, member) for member in range(len(shards))]
@@ -478,26 +474,27 @@
                 waiting.clear()
                 groups += 1
 
-        def quarter_of(quarter, *operands, **named):
-            nonlocal unit, state, rides
-            rides += unit is not None
-            ride = (unit, state, rides)
-            dzs, unit, state, shard = stage(quarter, *operands, ride=ride, **named)
-            if shard is not None:
-                collect(shard)
-            return dzs
+        def numbered(kernel, *operands, **named):
+            nonlocal rides
+            results = kernel(*operands, rides, **named)
+            rides += 1
+            if results[-1] is not None:
+                collect(results[-1])
+            return results[:-1]
 
         dz_three = None
         for quarter in range(4):
-            dz_three = quarter_of(quarter, mids, (g_one, g_two), w_four, w_pre=w_three, passed=dz_three)
-        dmid = (through(dz_three[0], w_three, g_one), through(dz_three[1], w_three, g_two))
-        dz_one = None
+            dz_three, unit, state = numbered(
+                stage, unit, state, quarter, mids, (g_one, g_two), w_four, w_pre=w_three, passed=dz_three)
+        dmid_one, state = numbered(last_stage, unit, state, dz_three[0], g_one, w_three)
+        dmid_two, _ = numbered(last_stage, None, state, dz_three[1], g_two, w_three)
+        dmid = (dmid_one, dmid_two)
+        dz_one = unit = state = None
         for quarter in range(4):
-            dz_one = quarter_of(quarter, (x_one, x_two), dmid, w_two, pres=pres, passed=dz_one)
-        dx_one, state, shard = last_stage(dz_one[0], dmid[0], w_one, unit, state, 8)
-        collect(shard)
-        dx_two, _, shard = last_stage(dz_one[1], dmid[1], w_one, None, state, 9)
-        collect(shard)
+            dz_one, unit, state = numbered(
+                stage, unit, state, quarter, (x_one, x_two), dmid, w_two, pres=pres, passed=dz_one)
+        dx_one, state = numbered(last_stage, unit, state, dz_one[0], dmid[0], w_one)
+        dx_two, _ = numbered(last_stage, None, state, dz_one[1], dmid[1], w_one)
         dx_one, dx_two = own_buffers(dx_one, dx_two)
         upper = lower = None
         for quarter in range(4):

time: 889 us -> 901 us (1.013)
  Pallas kernels: 646 us -> 705 us
  matrix products: 48.4 us -> 0 us
    pallas_call x2 -> x4, Pallas kernels: 83.7 us -> 150 us  [last_stage(): pl.pallas_call(functools.partial(last_kernel, early), grid=(rows // DX_RO...]
    dot_general x2 -> x0, matrix products: 48.4 us -> none  [mat_nt(): lax.dot_general(left_op, right_op, (((1,), (1,)), ((), ())), preferred_el...]
  transfers between devices with their start and end apart: 7 -> 7, of which waited for: 4 -> 4; matrix products, arithmetic and copies ran while one was open for 6% -> 0% of each run, Pallas kernels for 43% -> 49%
where the time goes in v3:
time: 901 us; the launch traced here: 893 us
  Pallas kernels  705 us (78%)
  waiting for transfers between devices  170 us (19%)
  between operations  14.4 us (2%)
    pallas_call x8, Pallas kernels, stage(): pl.pallas_call(functools.partial(stage_kernel, unit is not None, state is...  396 us
    all_gather x7, waiting for transfers between devices, gather(): whole = lax.all_gather(jnp.stack(shards, axis=1), AXES, axis=0, tiled=True)  168 us
    pallas_call x4, Pallas kernels, last_stage(): pl.pallas_call(functools.partial(last_kernel, early), grid=(rows // DX_RO...  150 us
    pallas_call x2, Pallas kernels, forward(): pl.pallas_call(forward_kernel, grid=(hidden // FORWARD_CHUNK,), out_shape...  91.5 us
    pallas_call x8, Pallas kernels, assemble(): pl.pallas_call(assemble_kernel, grid=(QUARTER,), out_shape=[jax.ShapeDtyp...  60.5 us
  transfers between devices with their start and end apart: 7, of which 4 were waited for; matrix products, arithmetic and copies ran while one was open for 0% of the time, Pallas kernels for 49%

profile of v3, /device:TPU:0, one launch (start us, length us, event | category | flops | bytes accessed | tf_op | source)
XLA Modules:
  0.0 892.8 jit_solution(11071832788679141455)
XLA Ops:
  7.2 0.0 all-gather.26.cloned.1.call-start
  7.2 45.8 %shard_map.127 = (bf16[2048,4096]{1,0:T(8,128)(2,1)}, bf16[2048,1024]{1,0:T(8,128)(2,1)}) custom-call(bf16[2048,1024]{1,0:T(8,128)(2,1)} %refs_0_.7, bf16[1024,4096]{1,0:T(8,128)(2,1)} %refs_2_.15, bf16[4096,1024]{1,0:T(8,128)(2,1)} %refs_4_.15), custom_call_target="tpu_custom_call" | custom-call | flops 34359738368 | bytes 41943040 | tf_op jit(solution)/shard_map/pallas_call | solution.py:394
  53.0 45.8 %shard_map.128 = (bf16[2048,4096]{1,0:T(8,128)(2,1)}, bf16[2048,1024]{1,0:T(8,128)(2,1)}) custom-call(bf16[2048,1024]{1,0:T(8,128)(2,1)} %refs_1_.11, bf16[1024,4096]{1,0:T(8,128)(2,1)} %refs_2_.15, bf16[4096,1024]{1,0:T(8,128)(2,1)} %refs_4_.15), custom_call_target="tpu_custom_call" | custom-call | flops 34359738368 | bytes 41943040 | tf_op jit(solution)/shard_map/pallas_call | solution.py:394
  98.8 49.0 %shard_map.129 = (bf16[2048,4096]{1,0:T(8,128)(2,1)}, bf16[2048,4096]{1,0:T(8,128)(2,1)}, f32[16,64,1024]{2,1,0:T(8,128)}, f32[16,64,1024]{2,1,0:T(8,128)}) custom-call(bf16[2048,1024]{1,0:T(8,128)(2,1)} %get-tuple-element.126.refs_0_, bf16[2048,1024]{1,0:T(8,128)(2,1)} %get-tuple-element.127.refs_1_, bf16[2048,1024]{1,0:T(8,128)(2,1)} %refs_1_.6, ...), custom_call_target="tpu_custom_call" | custom-call | flops 34359738368 | bytes 50331648 | tf_op jit(solution)/shard_map/pallas_call | solution.py:298
  147.7 55.2 %shard_map.130 = (bf16[2048,4096]{1,0:T(8,128)(2,1)}, bf16[2048,4096]{1,0:T(8,128)(2,1)}, f32[16,64,1024]{2,1,0:T(8,128)}, f32[16,64,1024]{2,1,0:T(8,128)}, f32[...) custom-call(bf16[2048,1024]{1,0:T(8,128)(2,1)} %get-tuple-element.12, ...), custom_call_target="tpu_custom_call", output_to_operand_aliasing={{0}: (8, {}), {1}: (9, {})} | custom-call | flops 34359738368 | bytes 50331648 | tf_op jit(solution)/shard_map/pallas_call | solution.py:298
  203.0 54.6 %shard_map.131 = (bf16[2048,4096]{1,0:T(8,128)(2,1)}, bf16[2048,4096]{1,0:T(8,128)(2,1)}, f32[16,64,1024]{2,1,0:T(8,128)}, f32[16,64,1024]{2,1,0:T(8,128)}, f32[...) custom-call(bf16[2048,1024]{1,0:T(8,128)(2,1)} %get-tuple-element.12, ...), custom_call_target="tpu_custom_call", output_to_operand_aliasing={{0}: (14, {}), {1}: (15, {})} | custom-call | flops 34359738368 | bytes 50331648 | tf_op jit(solution)/shard_map/pallas_call | solution.py:298
  257.6 0.0 all-gather.26.cloned.1.call-update
  257.6 0.0 all-gather.18.cloned.1.call-start
  257.7 56.1 %shard_map.132 = (bf16[2048,4096]{1,0:T(8,128)(2,1)}, bf16[2048,4096]{1,0:T(8,128)(2,1)}, f32[16,64,1024]{2,1,0:T(8,128)}, f32[16,64,1024]{2,1,0:T(8,128)}, f32[...) custom-call(bf16[2048,1024]{1,0:T(8,128)(2,1)} %get-tuple-element.12, ...), custom_call_target="tpu_custom_call", output_to_operand_aliasing={{0}: (14, {}), {1}: (15, {})} | custom-call | flops 34359738368 | bytes 50331648 | tf_op jit(solution)/shard_map/pallas_call | solution.py:298
  313.8 40.0 %shard_map.133 = (bf16[2048,1024]{1,0:T(8,128)(2,1)}, f32[2,2,40,1024]{3,2,1,0:T(8,128)}, f32[2,2,24,1024]{3,2,1,0:T(8,128)}, f32[2,2,40,1024]{3,2,1,0:T(8,128)}...) custom-call(bf16[2048,4096]{1,0:T(8,128)(2,1)} %get-tuple-element.15, ...), custom_call_target="tpu_custom_call" | custom-call | flops 17179869184 | bytes 33554432 | tf_op jit(solution)/shard_map/pallas_call | solution.py:348
  353.8 25.9 %shard_map.134 = (bf16[2048,1024]{1,0:T(8,128)(2,1)}, f32[1,2,64,1024]{3,2,1,0:T(8,128)}) custom-call(bf16[2048,4096]{1,0:T(8,128)(2,1)} %get-tuple-element.162.refs_0_, bf16[2048,1024]{1,0:T(8,128)(2,1)} %refs_1_.7, bf16[1024,4096]{1,0:T(8,128)(2,1)} %refs_2_.13, f32[2,2,40,1024]{3,2,1,0:T(8,128)} %get-tuple-element.163.refs_3_, ...), custom_call_target="tpu_custom_call" | custom-call | flops 17179869184 | bytes 33554432 | tf_op jit(solution)/shard_map/pallas_call | solution.py:348
  379.7 38.5 %shard_map.135 = (bf16[2048,4096]{1,0:T(8,128)(2,1)}, bf16[2048,4096]{1,0:T(8,128)(2,1)}, f32[16,64,1024]{2,1,0:T(8,128)}, f32[16,64,1024]{2,1,0:T(8,128)}) custom-call(bf16[2048,1024]{1,0:T(8,128)(2,1)} %refs_0_.7, bf16[2048,1024]{1,0:T(8,128)(2,1)} %refs_1_.11, bf16[2048,1024]{1,0:T(8,128)(2,1)} %get-tuple-element.161.refs_2_.refs_1_, ...), custom_call_target="tpu_custom_call" | custom-call | flops 25769803776 | bytes 50331648 | tf_op jit(solution)/shard_map/pallas_call | solution.py:298
  418.3 43.2 %shard_map.136 = (bf16[2048,4096]{1,0:T(8,128)(2,1)}, bf16[2048,4096]{1,0:T(8,128)(2,1)}, f32[16,64,1024]{2,1,0:T(8,128)}, f32[16,64,1024]{2,1,0:T(8,128)}, f32[...) custom-call(bf16[2048,1024]{1,0:T(8,128)(2,1)} %refs_0_.7, ...), custom_call_target="tpu_custom_call", output_to_operand_aliasing={{0}: (9, {}), {1}: (10, {})} | custom-call | flops 25769803776 | bytes 50331648 | tf_op jit(solution)/shard_map/pallas_call | solution.py:298
  461.5 43.7 %shard_map.137 = (bf16[2048,4096]{1,0:T(8,128)(2,1)}, bf16[2048,4096]{1,0:T(8,128)(2,1)}, f32[16,64,1024]{2,1,0:T(8,128)}, f32[16,64,1024]{2,1,0:T(8,128)}, f32[...) custom-call(bf16[2048,1024]{1,0:T(8,128)(2,1)} %refs_0_.7, ...), custom_call_target="tpu_custom_call", output_to_operand_aliasing={{0}: (15, {}), {1}: (16, {})} | custom-call | flops 25769803776 | bytes 50331648 | tf_op jit(solution)/shard_map/pallas_call | solution.py:298
  505.2 0.0 all-gather.18.cloned.1.call-update
  505.3 0.0 all-gather.24.cloned.1.call-start
  505.3 0.7 all-gather.24.cloned.1.call-update
  506.0 0.0 all-gather.22.cloned.1.call-start
  506.1 0.5 all-gather.22.cloned.1.call-update
  506.6 0.0 all-gather.20.cloned.1.call-start
  506.6 0.5 all-gather.20.cloned.1.call-update
  507.2 0.0 all-gather.16.cloned.1.call-start
  507.2 55.7 %shard_map.138 = (bf16[2048,4096]{1,0:T(8,128)(2,1)}, bf16[2048,4096]{1,0:T(8,128)(2,1)}, f32[16,64,1024]{2,1,0:T(8,128)}, f32[16,64,1024]{2,1,0:T(8,128)}, f32[...) custom-call(bf16[2048,1024]{1,0:T(8,128)(2,1)} %refs_0_.7, ...), custom_call_target="tpu_custom_call", output_to_operand_aliasing={{0}: (15, {}), {1}: (16, {})} | custom-call | flops 25769803776 | bytes 50331648 | tf_op jit(solution)/shard_map/pallas_call | solution.py:298
  563.0 0.0 all-gather.16.cloned.1.call-update
  563.0 0.0 all-gather.14.cloned.1.call-start
  563.0 49.8 %shard_map.139 = (bf16[2048,1024]{1,0:T(8,128)(2,1)}, f32[2,2,40,1024]{3,2,1,0:T(8,128)}, f32[2,2,24,1024]{3,2,1,0:T(8,128)}, f32[2,2,40,1024]{3,2,1,0:T(8,128)}...) custom-call(bf16[2048,4096]{1,0:T(8,128)(2,1)} %get-tuple-element.19, ...), custom_call_target="tpu_custom_call" | custom-call | flops 17179869184 | bytes 33554432 | tf_op jit(solution)/shard_map/pallas_call | solution.py:348
  612.9 34.5 %shard_map.140 = (bf16[2048,1024]{1,0:T(8,128)(2,1)}, f32[1,2,64,1024]{3,2,1,0:T(8,128)}) custom-call(bf16[2048,4096]{1,0:T(8,128)(2,1)} %get-tuple-element.206.refs_0_, bf16[2048,1024]{1,0:T(8,128)(2,1)} %get-tuple-element.169.refs_3_.refs_1_, bf16[1024,4096]{1,0:T(8,128)(2,1)} %refs_2_.15, f32[2,2,40,1024]{3,2,1,0:T(8,128)} %get-tuple-element.207.refs_3_, ...), custom_call_target="tpu_custom_call" | custom-call | flops 17179869184 | bytes 33554432 | tf_op jit(solution)/shard_map/pallas_call | solution.py:348
  647.4 2.4 pad_maximum_fusion
  649.8 0.0 all-gather.14.cloned.1.call-update
  649.9 7.0 shard_map.148
  656.9 0.0 all-gather.26.cloned.1.call-done
  656.9 7.7 shard_map.144
  664.5 0.0 all-gather.18.cloned.1.call-done
  664.5 8.2 shard_map.141
  672.7 0.0 all-gather.24.cloned.1.call-done
  672.7 7.5 shard_map.145
  680.1 9.7 %all-gather.22.cloned.1.call-done = f32[16,2,64,1024]{3,2,1,0:T(8,128)} async-done(((f32[1,2,64,1024]{3,2,1,0:T(8,128)}), f32[16,2,64,1024]{3,2,1,0:T(8,128)}) %all-gather.22.cloned.1.call-update) | async-done | bytes 8388624 | tf_op jit(solution)/shard_map/all_gather | solution.py:458
  689.9 7.4 shard_map.146
  697.3 43.7 %all-gather.20.cloned.1.call-done = f32[16,2,64,1024]{3,2,1,0:T(8,128)} async-done(((f32[1,2,64,1024]{3,2,1,0:T(8,128)}), f32[16,2,64,1024]{3,2,1,0:T(8,128)}) %all-gather.20.cloned.1.call-update) | async-done | bytes 8388624 | tf_op jit(solution)/shard_map/all_gather | solution.py:458
  741.0 7.4 shard_map.147
  748.4 43.7 %all-gather.16.cloned.1.call-done = f32[16,2,64,1024]{3,2,1,0:T(8,128)} async-done(((f32[1,2,64,1024]{3,2,1,0:T(8,128)}), f32[16,2,64,1024]{3,2,1,0:T(8,128)}) %all-gather.16.cloned.1.call-update) | async-done | bytes 8388624 | tf_op jit(solution)/shard_map/all_gather | solution.py:458
  792.1 7.4 shard_map.142
  799.6 71.3 %all-gather.14.cloned.1.call-done.refs_0_ = f32[16,2,2,64,1024]{4,3,2,1,0:T(8,128)} async-done(((f32[1,2,2,64,1024]{4,3,2,1,0:T(8,128)}), f32[16,2,2,64,1024]{4,3,2,1,0:T(8,128)}) %all-gather.14.cloned.1.call-update) | async-done | bytes 16777232 | tf_op jit(solution)/shard_map/all_gather | solution.py:458
  870.9 7.4 shard_map.143
  878.3 7.4 shard_map.149
Async XLA Ops:
  7.2 649.7 %all-gather.26.cloned.1.call-start = ((), (), s32[]{:S(2)}) async-start(), calls=%async_computation.6 | async-start | bytes 8912896 | tf_op jit(solution)/shard_map/all_gather | solution.py:458
  257.6 406.9 %all-gather.18.cloned.1.call-start = ((), (), s32[]{:S(2)}) async-start(), calls=%async_computation.2 | async-start | bytes 8912896 | tf_op jit(solution)/shard_map/all_gather | solution.py:458
  505.3 167.4 %all-gather.24.cloned.1.call-start = ((), (), s32[]{:S(2)}) async-start(), calls=%async_computation.5 | async-start | bytes 8912896 | tf_op jit(solution)/shard_map/all_gather | solution.py:458
  506.0 183.9 %all-gather.22.cloned.1.call-start = ((), (), s32[]{:S(2)}) async-start(), calls=%async_computation.4 | async-start | bytes 8912896 | tf_op jit(solution)/shard_map/all_gather | solution.py:458
  506.6 234.4 %all-gather.20.cloned.1.call-start = ((), (), s32[]{:S(2)}) async-start(), calls=%async_computation.3 | async-start | bytes 8912896 | tf_op jit(solution)/shard_map/all_gather | solution.py:458
  507.2 285.0 %all-gather.16.cloned.1.call-start = ((), (), s32[]{:S(2)}) async-start(), calls=%async_computation.1 | async-start | bytes 8912896 | tf_op jit(solution)/shard_map/all_gather | solution.py:458
  563.0 307.9 %all-gather.14.cloned.1.call-start = ((), (), s32[]{:S(2)}) async-start(), calls=%async_computation | async-start | bytes 17825792 | tf_op jit(solution)/shard_map/all_gather | solution.py:458
Sparse Core Ops, SparseCore 0:
  257.7 64.5 all-gather.25
  505.4 63.5 all-gather.17
  571.2 66.6 all-gather.23
  640.0 49.7 all-gather.21
  692.0 48.9 all-gather.19
  743.1 48.9 all-gather.15
  794.4 76.4 all-gather.13
